TPU v7x, 32 devices: a whole 2x2x4 slice. The times are simulated.
32 devices in a mesh: dom: 8 (over y, x, core), sub: 4 (over z).
Axes of the slice: x: 2, y: 2, z: 4, core: 2. Of those that a mesh axis runs over, the one named last changes fastest.
Arguments:
- displacement: float32 [3, 43200], P(None, ('dom', 'sub')), may hold values from -0.01 to 0.01
- velocity: float32 [3, 43200], P(None, ('dom', 'sub')), may hold values from -3 to 3
- energy: float32 [27, 1536], P(None, ('dom', 'sub')), may hold values from 0.5 to 18, as said below
- mass_density: float32 [125, 1536], P(None, ('dom', 'sub')), may hold values from 0.5 to 4
- live_mask: int32 [1536], P(('dom', 'sub')), may hold values from 0 to 1, as said below
- time_step: float32 [], replicated, may hold values from 0.004 to 0.008
Outputs:
- new_velocity: float32 [3, 43200], P(None, ('dom', 'sub'))
- energy_rate: float32 [27, 1536], P(None, ('dom', 'sub'))
- mesh_velocity: float32 [3, 43200], P(None, ('dom', 'sub'))
Inputs may be any that keep to these rules, and one draw needn't show every extreme that they name: `energy`: internal energies are positive. `live_mask`: at most 36 element slots of one device are live, and some device has exactly 36.
All inputs are finite; a program needn't handle non-finite values.
Results may differ from a plain program's by a relative error of at most 0.0003.
Values sent between devices are 32-bit elements; how exact they have to be, the bound alone decides.
A program may use at most 64 MiB of HBM per device.

v0:
```python
import functools
import math

import jax
import jax.numpy as jnp
import numpy as np
from jax import lax
from jax.experimental import pallas as pl
from jax.experimental.pallas import tpu as pltpu
from jax.sharding import PartitionSpec as P

EX = 1
EY = 8
EZ = 6
ELEMS = EX * EY * EZ
HALF = 64

adiabatic = 5.0 / 3.0
viscosity = 0.3
mesh_step = 0.01
MESH = pl.DeviceIdType.MESH
STEPS = [(dx, dz) for dx in (-1, 0, 1) for dz in (-1, 0, 1) if (dx, dz) != (0, 0)]


def one_dimension():
    root_term = math.sqrt(10.0 / 7.0)
    outer_root = math.sqrt(5.0 + 2.0 * root_term) / 3.0
    inner_root = math.sqrt(5.0 - 2.0 * root_term) / 3.0
    gauss_roots = np.array([-outer_root, -inner_root, 0.0, inner_root, outer_root])
    outer_weight = (322.0 - 13.0 * math.sqrt(70.0)) / 900.0
    middle_weight = (322.0 + 13.0 * math.sqrt(70.0)) / 900.0
    weights = (
        np.array([outer_weight, middle_weight, 128.0 / 225.0, middle_weight, outer_weight]) / 2.0
    )
    points = (1.0 + gauss_roots) / 2.0
    lobatto = [0.0, (1.0 - 1.0 / math.sqrt(5.0)) / 2.0, (1.0 + 1.0 / math.sqrt(5.0)) / 2.0, 1.0]
    values = np.ones((5, 4))
    slopes = np.zeros((5, 4))
    for node in range(4):
        for other in range(4):
            if other != node:
                values[:, node] *= (points - lobatto[other]) / (lobatto[node] - lobatto[other])
                term = np.ones(5) / (lobatto[node] - lobatto[other])
                for third in range(4):
                    if third != node and third != other:
                        term = term * (points - lobatto[third]) / (lobatto[node] - lobatto[third])
                slopes[:, node] += term
    bernstein = np.stack([(1.0 - points) ** 2, 2.0 * points * (1.0 - points), points**2], axis=1)
    return values, slopes, bernstein, weights


def outer_triple(first, second, third):
    product = np.einsum("ia,jb,kc->ijkabc", first, second, third)
    return product.reshape(125, -1)


def halves(table, rows):
    padded = np.concatenate([table, np.repeat(table[-1:], 3, axis=0)], axis=0)
    padded = np.pad(padded, [(0, 0), (0, rows - table.shape[1])])
    return np.concatenate([padded[:64], padded[64:]], axis=1)


@functools.lru_cache(None)
def tables():
    values, slopes, bernstein, weights = one_dimension()
    basis = halves(outer_triple(values, values, values), 64)
    grad = np.concatenate(
        [
            halves(outer_triple(slopes, values, values), 64),
            halves(outer_triple(values, slopes, values), 64),
            halves(outer_triple(values, values, slopes), 64),
        ],
        axis=0,
    )
    energy = halves(outer_triple(bernstein, bernstein, bernstein), 32)
    forward = np.concatenate([grad, basis], axis=0)
    backward = np.zeros((128, 384))
    backward[:, :192] = grad.T
    backward[:, 256:320] = basis.T
    energy_pair = np.concatenate([energy, energy.T], axis=1)
    weight = np.einsum("i,j,k->ijk", weights, weights, weights).reshape(125)
    weight = np.pad(weight, (0, 3))
    spread_weight = np.zeros((64, 128))
    spread_weight[:, :ELEMS] = weight[:64, None]
    spread_weight[:, 64 : 64 + ELEMS] = weight[64:, None]
    planes_y, planes_z = 3 * EY + 1, 3 * EZ
    pick = np.zeros((planes_y * planes_z, 16 * HALF), np.float32)
    for b in range(4):
        for c in range(4):
            for q in range(EY):
                for r in range(EZ):
                    z = 3 * r + c - 1
                    if z >= 0:
                        lane = (4 * b + c) * HALF + q * EZ + r
                        pick[(3 * q + b) * planes_z + z, lane] = 1.0
    return [np.asarray(t, np.float32) for t in (forward, backward, energy_pair, spread_weight)] + [
        pick
    ]


def dot(left, right):
    left_high, left_low = split_two(left)
    right_high, right_low = split_two(right)
    product = functools.partial(jnp.dot, preferred_element_type=jnp.float32)
    return (
        product(left_low, right_high) + product(left_high, right_low)
    ) + product(left_high, right_high)


def split_two(value):
    high = value.astype(jnp.bfloat16)
    return high, (value - high.astype(jnp.float32)).astype(jnp.bfloat16)


def cofactors(m):
    return [
        [
            m[(i + 1) % 3][(j + 1) % 3] * m[(i + 2) % 3][(j + 2) % 3]
            - m[(i + 1) % 3][(j + 2) % 3] * m[(i + 2) % 3][(j + 1) % 3]
            for j in range(3)
        ]
        for i in range(3)
    ]


def turn(value, rows, lanes):
    if rows:
        value = pltpu.roll(value, rows % value.shape[0], 0)
    if lanes % value.shape[1]:
        value = pltpu.roll(value, lanes % value.shape[1], 1)
    return value


def split_three(value):
    high = value.astype(jnp.bfloat16).astype(jnp.float32)
    rest = value - high
    middle = rest.astype(jnp.bfloat16).astype(jnp.float32)
    return jnp.concatenate([high, middle, rest - middle], axis=0).astype(jnp.bfloat16)


def kernel(
    n_dom,
    n_sub,
    disp_in,
    vel_in,
    energy_in,
    density_in,
    live_in,
    step_in,
    forward,
    backward,
    energy_pair,
    quad_weight,
    pick,
    new_vel_out,
    rate_out,
    mesh_vel_out,
    flat,
    wide,
    first,
    local,
    state,
    out_nodes,
    out_wide,
    density_pad,
    energy_pad,
    live_pad,
    packs,
    x_first,
    x_got,
    z_got,
    d_got,
    sum_dom,
    sum_sub,
    send_sems,
    recv_sems,
    dom_send,
    dom_recv,
    sub_send,
    sub_recv,
):
    dom = lax.axis_index("dom")
    sub = lax.axis_index("sub")
    plane = (3 * EY + 1) * 3 * EZ

    def inside(dx, dz):
        ok = None
        for step, place, size in ((dx, dom, n_dom), (dz, sub, n_sub)):
            if step:
                here = (place > 0) if step < 0 else (place < size - 1)
                ok = here if ok is None else jnp.logical_and(ok, here)
        return ok

    x_first[...] = jnp.zeros_like(x_first)
    x_got[...] = jnp.zeros_like(x_got)
    z_got[...] = jnp.zeros_like(z_got)
    d_got[...] = jnp.zeros_like(d_got)

    barrier = pltpu.get_barrier_semaphore()
    one_phase = n_dom * n_sub <= 64
    if one_phase:
        devices = n_dom * n_sub
        count = devices - 1

        @pl.loop(1, devices, unroll=True)
        def _(i):
            t = lax.rem(dom * n_sub + sub + i, devices)
            pl.semaphore_signal(
                barrier,
                inc=1,
                device_id=(t // n_sub, lax.rem(t, n_sub)),
                device_id_type=MESH,
            )

    else:
        count = (n_dom - 1) + (n_sub - 1)
        for dx, dz in STEPS:
            if dx and dz:
                ok = inside(dx, dz)
                count = count + ok.astype(jnp.int32)

                @pl.when(ok)
                def _():
                    pl.semaphore_signal(
                        barrier, inc=1, device_id=(dom + dx, sub + dz), device_id_type=MESH
                    )

        @pl.loop(1, n_dom)
        def _(i):
            pl.semaphore_signal(
                barrier, inc=1, device_id=(lax.rem(dom + i, n_dom), sub), device_id_type=MESH
            )

        @pl.loop(1, n_sub)
        def _(i):
            pl.semaphore_signal(
                barrier, inc=1, device_id=(dom, lax.rem(sub + i, n_sub)), device_id_type=MESH
            )

    first[...] = jnp.zeros_like(first)
    density_pad[...] = jnp.zeros_like(density_pad)
    energy_pad[...] = jnp.zeros_like(energy_pad)
    live_pad[...] = jnp.zeros_like(live_pad)
    flat[...] = jnp.zeros_like(flat)
    out_wide[...] = jnp.zeros_like(out_wide)

    lane = lax.broadcasted_iota(jnp.int32, (64, 128), 1)
    row = lax.broadcasted_iota(jnp.int32, (64, 128), 0)
    q_of, r_of = lane // EZ, lane % EZ
    a_of, b_of, c_of = row // 16, (row // 4) % 4, row % 4
    valid = lane < ELEMS
    triple = lambda x: jnp.concatenate([x, x, x], axis=0)
    y_up = triple((b_of == 3) & (q_of < EY - 1) & valid)
    y_down = triple((b_of == 0) & (q_of > 0) & valid)
    z_up = triple((c_of == 3) & (r_of < EZ - 1) & valid)
    z_down = triple((c_of == 0) & (r_of > 0) & valid)
    off_wall = jnp.where(
        valid
        & jnp.logical_or(a_of > 0, dom > 0)
        & jnp.logical_or(jnp.logical_or(c_of > 0, r_of > 0), sub > 0),
        1.0,
        0.0,
    )
    off_wall = triple(off_wall)
    owned = jnp.where(
        valid & (a_of > 0) & (c_of > 0) & ((b_of < 3) | (q_of == EY - 1)), 1.0, 0.0
    )
    owned = triple(owned)
    lane16, row16 = lane[:16], row[:16]
    r16 = jnp.where(lane16 < ELEMS, lane16 % EZ, EZ)

    flat[0:3, :] = disp_in[...]
    flat[3:6, :] = vel_in[...]
    stacked = jnp.concatenate([flat[:, plane * x : plane * (x + 1)] for x in range(3)], axis=0)
    picked = jnp.dot(split_three(stacked), pick[...], preferred_element_type=jnp.float32)
    wide[...] = picked[0:24] + picked[24:48] + picked[48:72]
    for x in range(3):
        for pair in range(8):
            got = wide[8 * x : 8 * x + 8, 128 * pair : 128 * pair + 128]
            other = turn(got, 0, 64)
            at = 16 * (x + 1) + 2 * pair
            keep = lane[:8] < 64
            first[pl.ds(at, 8, stride=64), :] = jnp.where(keep, got, 0.0)
            first[pl.ds(at + 1, 8, stride=64), :] = jnp.where(keep, other, 0.0)

    pl.semaphore_wait(barrier, count)

    def faces(source, fields, place, shifts):
        packed = jnp.zeros((16, 128), jnp.float32)
        for k in range(fields):
            face = source[pl.ds(64 * k + place, 16, stride=4), :]
            if place == 3:
                packed = jnp.where(r16 == EZ - 1 - k, turn(face, 0, -k), packed)
            else:
                packed = jnp.where(r16 == k, turn(face, 0, k), packed)
        return packed

    waits = []

    def exchange_start(rnd, source, fields, x_target, ups, downs):
        if ups:
            packs[rnd, 1] = faces(source, fields, 3, None)
        if downs:
            packs[rnd, 0] = faces(source, fields, 0, None)
        started = []
        for number, (dx, dz) in enumerate(STEPS):
            lead = dz if dz else dx
            going = (dx, dz)
            up = all(s >= 0 for s in going)
            down = all(s <= 0 for s in going)
            if not ((ups and downs) or (ups and up) or (downs and down)):
                continue
            target = (dom + dx, sub + dz)
            jobs = []
            if dz == 0:
                base = 48 if dx > 0 else 0
                slot = 0 if dx > 0 else 1
                jobs.append(
                    (
                        source_blocks(source, fields, base),
                        x_target(slot),
                    )
                )
            elif dx == 0:
                side = 1 if dz > 0 else 0
                jobs.append((packs.at[rnd, side], z_got.at[rnd, 1 - side]))
            else:
                side = 1 if dz > 0 else 0
                half = 8 if dx > 0 else 0
                slot = (0 if dx > 0 else 1) + 2 * (1 - side)
                jobs.append((packs.at[rnd, side, pl.ds(half, 8)], d_got.at[rnd, slot]))
            src, dst = jobs[0]
            copy = pltpu.make_async_remote_copy(
                src_ref=src,
                dst_ref=dst,
                send_sem=send_sems.at[rnd, number],
                recv_sem=recv_sems.at[rnd, number],
                device_id=target,
                device_id_type=MESH,
            )

            @pl.when(inside(dx, dz))
            def _():
                copy.start()

            started.append((copy, (dx, dz)))
        return started

    def source_blocks(source, fields, base):
        blocks = source.reshape(source.shape[0] // 64, 64, 128)
        return blocks.at[pl.ds(0, fields), pl.ds(base, 16)]

    def exchange_wait(started):
        for copy, (dx, dz) in started:

            @pl.when(inside(-dx, -dz))
            def _():
                copy.wait_recv()

        waits.extend(started)

    def exchange_add(rnd, source, target, fields, x_from, ups, downs):
        if target is not source:
            target[...] = source[...]
        top = lax.broadcasted_iota(jnp.int32, (8, 128), 0) < 4
        for came, side, place in ((ups, 0, 0), (downs, 1, 3)):
            if not came:
                continue
            face = z_got[rnd, side]
            low = jnp.where(top, turn(d_got[rnd, 2 * side], 4, 0), 0.0)
            high = jnp.where(top, 0.0, turn(d_got[rnd, 2 * side + 1], 4, 0))
            face = face + jnp.concatenate([low, high], axis=0)
            for k in range(fields):
                if place == 0:
                    part = jnp.where(r16 == 0, turn(face, 0, k - (EZ - 1)), 0.0)
                else:
                    part = jnp.where(r16 == EZ - 1, turn(face, 0, EZ - 1 - k), 0.0)
                at = pl.ds(64 * k + place, 16, stride=4)
                target[at, :] = target[at, :] + part
        for k in range(fields):
            if ups:
                target[64 * k : 64 * k + 16, :] += x_from(0)[k]
            if downs:
                target[64 * k + 48 : 64 * k + 64, :] += x_from(1)[k]

    started = exchange_start(0, first, 6, lambda slot: x_first, True, False)

    step = step_in[0, 0]
    density_pad[0:ELEMS, 0:125] = density_in[...]
    energy_pad[0:27, 0:ELEMS] = energy_in[...]
    live_pad[0:1, 0:ELEMS] = live_in[...].astype(jnp.float32)
    live = live_pad[0:1, :]
    live = live + turn(live, 0, 64)
    by_point = jnp.transpose(density_pad[...])
    mass_density = by_point[0:64] + turn(by_point[64:128], 0, 64)
    weight = quad_weight[...]
    live_weight = weight * live
    mass_weight = live_weight * mass_density
    energy_pad_v = energy_pad[...]
    at_points = dot(
        energy_pair[:, 0:64], jnp.concatenate([energy_pad_v, turn(energy_pad_v, 0, 64)], axis=0)
    )

    def paired(v):
        return jnp.concatenate(
            [
                jnp.concatenate([v[64 * k : 64 * k + 64], turn(v[64 * k : 64 * k + 64], 0, 64)], 0)
                for k in range(v.shape[0] // 64)
            ],
            axis=1,
        )

    def folded(product):
        half = product.shape[0] // 2
        out = []
        for k in range(product.shape[1] // 128):
            part = product[:, 128 * k : 128 * k + 128]
            out.append(part[:half] + turn(part[half:], 0, 64))
        return out

    def gradient(v):
        shaped = dot(forward[0:192, :], paired(v))
        return [
            [shaped[64 * m : 64 * m + 64, 128 * c : 128 * c + 128] for m in range(3)]
            for c in range(3)
        ]

    def jacobian_of(v):
        jacobian = gradient(v)
        for c in range(3):
            jacobian[c][c] = jacobian[c][c] + 1.0
        return jacobian

    def project(fields):
        right = jnp.concatenate(
            [jnp.concatenate([fields[c][m] for c in range(3)], axis=1) for m in range(3)], axis=0
        )
        return share(jnp.concatenate(folded(dot(backward[:, 0:192], right)), axis=0))

    def share(v):
        v = v * jnp.where(triple(valid), 1.0, 0.0)
        v = v + jnp.where(y_up, turn(v, 12, -EZ), 0.0) + jnp.where(y_down, turn(v, -12, EZ), 0.0)
        v = v + jnp.where(z_up, turn(v, 3, -1), 0.0) + jnp.where(z_down, turn(v, -3, 1), 0.0)
        return v

    def interpolate(v):
        return dot(forward[192:256, :], paired(v))

    def volume_of(jacobian, cofactor):
        return (
            jacobian[0][0] * cofactor[0][0]
            + jacobian[0][1] * cofactor[0][1]
            + jacobian[0][2] * cofactor[0][2]
        )

    def begin(rnd, v, ups=True, downs=True):
        source = local.at[rnd - 1]
        source[...] = v
        return exchange_start(rnd, source, 3, lambda slot: x_got.at[rnd - 1, slot], ups, downs)

    def finish(rnd, started, ups=True, downs=True):
        exchange_wait(started)
        source = local.at[rnd - 1]
        exchange_add(
            rnd, source, state, 3, lambda slot: x_got.at[rnd - 1, slot], ups, downs
        )
        return state[...] * off_wall

    exchange_wait(started)
    out_nodes[...] = first[0:384, :]
    exchange_add(0, out_nodes, out_nodes, 6, lambda slot: x_first, True, False)
    displacement = out_nodes[0:192, :]
    velocity = out_nodes[192:384, :]

    jacobian = jacobian_of(displacement)
    velocity_grad = gradient(velocity)
    cofactor = cofactors(jacobian)
    volume = volume_of(jacobian, cofactor)
    inverse = 1.0 / volume
    density = mass_density * inverse
    pressure = (adiabatic - 1.0) * density * at_points
    spatial = [
        [
            (
                velocity_grad[c][0] * cofactor[m][0]
                + velocity_grad[c][1] * cofactor[m][1]
                + velocity_grad[c][2] * cofactor[m][2]
            )
            * inverse
            for m in range(3)
        ]
        for c in range(3)
    ]
    viscous = viscosity * density
    stress = [[None] * 3 for _ in range(3)]
    for c in range(3):
        for m in range(c, 3):
            value = viscous * (spatial[c][m] + spatial[m][c])
            stress[c][m] = stress[m][c] = value - pressure if c == m else value
    flux = [
        [
            -live_weight
            * (
                stress[c][0] * cofactor[0][m]
                + stress[c][1] * cofactor[1][m]
                + stress[c][2] * cofactor[2][m]
            )
            for m in range(3)
        ]
        for c in range(3)
    ]
    started = begin(1, project(flux))
    power = stress[0][0] * spatial[0][0]
    for c in range(3):
        for m in range(3):
            if c + m > 0:
                power = power + stress[c][m] * spatial[c][m]
    power = live_weight * volume * power
    sums = folded(
        dot(energy_pair[:, 64:128], jnp.concatenate([power, weight * mass_density], axis=1))
    )
    rate_out[...] = (sums[0] / sums[1])[0:27, 0:ELEMS]
    force = finish(1, started)

    wide_mass = jnp.concatenate([mass_weight] * 3, axis=1)
    values = interpolate(force)
    weighted = wide_mass * values
    image = share(jnp.concatenate(folded(dot(backward[:, 256:320], weighted)), axis=0))
    started = begin(2, image)

    def total(x):
        return jnp.sum(jnp.sum(x, axis=0, keepdims=True), axis=1, keepdims=True)

    norm_part = total(force * force * owned)
    product_part = total(weighted * values)
    image = finish(2, started)
    image_norm_part = total(image * image * owned)
    values = interpolate(image)
    image_product_part = total(wide_mass * values * values)

    lane1 = lane[0:1]
    packed = jnp.where(
        lane1 == 0,
        norm_part,
        jnp.where(
            lane1 == 1,
            product_part,
            jnp.where(lane1 == 2, image_norm_part, image_product_part),
        ),
    )

    late = []

    def all_sum(value, slots, size, place, target, sends, recvs):
        slots[0] = value

        def copy_of(i):
            return pltpu.make_async_remote_copy(
                src_ref=slots.at[0],
                dst_ref=slots.at[i],
                send_sem=sends.at[i],
                recv_sem=recvs.at[i],
                device_id=target(lax.rem(place + i, size)),
                device_id_type=MESH,
            )

        @pl.loop(1, size, unroll=True)
        def _(i):
            copy_of(i).start()

        @pl.loop(1, size, unroll=True)
        def _(i):
            copy_of(i).wait_recv()

        out = jnp.sum(slots[...], axis=0)

        late.append((copy_of, size))
        return out

    if one_phase:
        packed = all_sum(
            packed,
            sum_dom,
            n_dom * n_sub,
            dom * n_sub + sub,
            lambda t: (t // n_sub, lax.rem(t, n_sub)),
            dom_send,
            dom_recv,
        )
    else:
        packed = all_sum(packed, sum_dom, n_dom, dom, lambda t: (t, sub), dom_send, dom_recv)
        packed = all_sum(packed, sum_sub, n_sub, sub, lambda t: (dom, t), sub_send, sub_recv)
    rr, rw, ww, wmw = (
        jnp.sum(jnp.where(lane1 == k, packed, 0.0), axis=1, keepdims=True) for k in range(4)
    )
    first_length = rr / rw
    next_norm = first_length * (first_length * ww) - rr
    conjugacy = next_norm / rr
    residual_image = rw - first_length * ww
    residual_product = rw - 2.0 * first_length * ww + first_length * first_length * wmw
    bend = residual_product + 2.0 * conjugacy * residual_image + conjugacy * conjugacy * rw
    second_length = next_norm / bend
    on_force = first_length + second_length * (1.0 + conjugacy)
    on_image = second_length * first_length
    new_velocity = velocity + step * (on_force * force - on_image * image)
    moved = displacement + step * new_velocity

    def shape(v):
        jacobian = jacobian_of(v)
        cofactor = cofactors(jacobian)
        volume = volume_of(jacobian, cofactor)
        norm_sq = None
        for c in range(3):
            for m in range(3):
                square = jacobian[c][m] * jacobian[c][m]
                norm_sq = square if norm_sq is None else norm_sq + square
        scale = live_weight * jnp.exp(jnp.log(volume) * (-2.0 / 3.0))
        along = scale * (2.0 / 3.0)
        across = scale * (2.0 / 9.0) * (norm_sq / volume)
        return project(
            [
                [along * jacobian[c][m] - across * cofactor[c][m] for m in range(3)]
                for c in range(3)
            ]
        )

    started = begin(3, shape(moved))
    slope = finish(3, started)
    started = begin(4, shape(moved - mesh_step * slope), False, True)
    last = finish(4, started, False, True)
    mesh_velocity = new_velocity - (mesh_step / step) * (slope + last)

    out_nodes[0:192, :] = new_velocity * owned
    out_nodes[192:384, :] = mesh_velocity * owned
    for x in range(3):
        for pair in range(8):
            at = 16 * (x + 1) + 2 * pair
            even = out_nodes[pl.ds(at, 6, stride=64), :]
            odd = out_nodes[pl.ds(at + 1, 6, stride=64), :]
            out_wide[8 * x : 8 * x + 6, 128 * pair : 128 * pair + 128] = even + turn(odd, 0, 64)
    back = lax.dot_general(
        split_three(out_wide[...]),
        pick[...],
        (((1,), (1,)), ((), ())),
        preferred_element_type=jnp.float32,
    )
    back = back[0:24] + back[24:48] + back[48:72]
    for x in range(3):
        new_vel_out[:, plane * x : plane * (x + 1)] = back[8 * x : 8 * x + 3]
        mesh_vel_out[:, plane * x : plane * (x + 1)] = back[8 * x + 3 : 8 * x + 6]

    for copy_of, size in late:

        @pl.loop(1, size, unroll=True)
        def _(i, copy_of=copy_of):
            copy_of(i).wait_send()

    for copy, (dx, dz) in waits:

        @pl.when(inside(dx, dz))
        def _():
            copy.wait_send()


def hand_on(*refs):
    for source, target in zip(refs[:3], refs[3:]):
        target[...] = source[...]


def body(n_dom, n_sub, displacement, velocity, energy, mass_density, live_mask, time_step):
    forward, backward, energy_pair, quad_weight, pick = tables()
    vmem = pl.BlockSpec(memory_space=pltpu.VMEM)
    smem = pl.BlockSpec(memory_space=pltpu.SMEM)
    f32 = jnp.float32
    nodes = displacement.shape[1]
    wide_sum = n_dom * n_sub if n_dom * n_sub <= 64 else n_dom
    made = pl.pallas_call(
        functools.partial(kernel, n_dom, n_sub),
        out_shape=(
            jax.ShapeDtypeStruct(displacement.shape, f32),
            jax.ShapeDtypeStruct(energy.shape, f32),
            jax.ShapeDtypeStruct(displacement.shape, f32),
        ),
        in_specs=[vmem] * 5 + [smem] + [vmem] * 5,
        out_specs=(vmem, vmem, vmem),
        scratch_shapes=[
            pltpu.VMEM((8, nodes), f32),
            pltpu.VMEM((24, 1024), f32),
            pltpu.VMEM((512, 128), f32),
            pltpu.VMEM((4, 192, 128), f32),
            pltpu.VMEM((192, 128), f32),
            pltpu.VMEM((384, 128), f32),
            pltpu.VMEM((24, 1024), f32),
            pltpu.VMEM((128, 128), f32),
            pltpu.VMEM((32, 128), f32),
            pltpu.VMEM((8, 128), f32),
            pltpu.VMEM((5, 2, 16, 128), f32),
            pltpu.VMEM((6, 16, 128), f32),
            pltpu.VMEM((4, 2, 3, 16, 128), f32),
            pltpu.VMEM((5, 2, 16, 128), f32),
            pltpu.VMEM((5, 4, 8, 128), f32),
            pltpu.VMEM((wide_sum, 1, 128), f32),
            pltpu.VMEM((n_sub, 1, 128), f32),
            pltpu.SemaphoreType.DMA((5, 8)),
            pltpu.SemaphoreType.DMA((5, 8)),
            pltpu.SemaphoreType.DMA((wide_sum,)),
            pltpu.SemaphoreType.DMA((wide_sum,)),
            pltpu.SemaphoreType.DMA((n_sub,)),
            pltpu.SemaphoreType.DMA((n_sub,)),
        ],
        compiler_params=pltpu.CompilerParams(collective_id=0, has_side_effects=True),
    )(
        displacement,
        velocity,
        energy,
        mass_density.T,
        live_mask.reshape(1, -1),
        time_step.reshape(1, 1),
        forward,
        backward,
        energy_pair,
        quad_weight,
        jnp.asarray(pick, jnp.bfloat16),
    )
    return pl.pallas_call(
        hand_on,
        out_shape=[jax.ShapeDtypeStruct(m.shape, f32) for m in made],
        in_specs=[vmem] * 3,
        out_specs=[vmem] * 3,
    )(*made)


def solution(mesh):
    split = ("dom", "sub")
    return jax.shard_map(
        functools.partial(body, mesh.shape["dom"], mesh.shape["sub"]),
        mesh=mesh,
        in_specs=(
            P(None, split),
            P(None, split),
            P(None, split),
            P(None, split),
            P(split),
            P(),
        ),
        out_specs=(P(None, split), P(None, split), P(None, split)),
        check_vma=False,
    )
```

profile of v0, /device:TPU:0, one launch (start us, length us, event | category | flops | bytes accessed | tf_op | source)
XLA Modules:
  0.0 37.7 jit_solution(17142757982162617391)
XLA Ops:
  1.3 35.1 %shard_map.130 = (f32[3,1350]{1,0:T(4,128)}, f32[27,48]{1,0:T(8,128)}, f32[3,1350]{1,0:T(4,128)}) custom-call(f32[3,1350]{1,0:T(4,128)} %disp_in.1, f32[3,1350]{1,0:T(4,128)} %vel_in.1, f32[27,48]{1,0:T(8,128)} %energy_in.1, f32[48,125]{1,0:T(8,128)} %bitcast.4, s32[1,48]{1,0:T(1,128)} %bitcast.5, f32[1,1]{1,0:T(1,128)} %bitcast.3.step_in, ...), custom_call_target="tpu_custom_call" | custom-call | tf_op jit(solution)/shard_map/pallas_call | solution.py:677
  36.3 1.4 %shard_map.131 = (f32[3,1350]{1,0:T(4,128)}, f32[27,48]{1,0:T(8,128)}, f32[3,1350]{1,0:T(4,128)}) custom-call(f32[3,1350]{1,0:T(4,128)} %get-tuple-element.6.refs_0_, f32[27,48]{1,0:T(8,128)} %get-tuple-element.7.refs_1_, f32[3,1350]{1,0:T(4,128)} %get-tuple-element.8.refs_2_), custom_call_target="tpu_custom_call" | custom-call | tf_op jit(solution)/shard_map/pallas_call | solution.py:725
where the time goes:
time: 38.1 us; the launch traced here: 37.7 us
  Pallas kernels  36.5 us (96%)
  between operations  1.29 us (3%)
    pallas_call x1, Pallas kernels, body(): pl.pallas_call(functools.partial(kernel, n_dom, n_sub), out_shape=(jax.Sh...  35.1 us
    pallas_call x1, Pallas kernels, body(): pl.pallas_call(hand_on, out_shape=[jax.ShapeDtypeStruct(m.shape, f32) for...  1.4 us

commit v1 on v0

--- a/solution.py
+++ b/solution.py
@@ -141,17 +141,17 @@
 def kernel(
     n_dom,
     n_sub,
-    disp_in,
-    vel_in,
-    energy_in,
-    density_in,
-    live_in,
-    step_in,
-    forward,
-    backward,
-    energy_pair,
-    quad_weight,
-    pick,
+    disp_in_hbm,
+    vel_in_hbm,
+    energy_in_hbm,
+    density_in_hbm,
+    live_in_hbm,
+    step_in_hbm,
+    forward_hbm,
+    backward_hbm,
+    energy_pair_hbm,
+    quad_weight_hbm,
+    pick_hbm,
     new_vel_out,
     rate_out,
     mesh_vel_out,
@@ -178,6 +178,18 @@
     dom_recv,
     sub_send,
     sub_recv,
+    disp_in,
+    vel_in,
+    energy_in,
+    density_in,
+    live_in,
+    step_in,
+    forward,
+    backward,
+    energy_pair,
+    quad_weight,
+    pick,
+    in_sems,
 ):
     dom = lax.axis_index("dom")
     sub = lax.axis_index("sub")
@@ -190,6 +202,26 @@
                 here = (place > 0) if step < 0 else (place < size - 1)
                 ok = here if ok is None else jnp.logical_and(ok, here)
         return ok
+
+    held = [
+        (disp_in_hbm, disp_in),
+        (vel_in_hbm, vel_in),
+        (pick_hbm, pick),
+        (forward_hbm, forward),
+        (backward_hbm, backward),
+        (density_in_hbm, density_in),
+        (energy_in_hbm, energy_in),
+        (live_in_hbm, live_in),
+        (energy_pair_hbm, energy_pair),
+        (quad_weight_hbm, quad_weight),
+        (step_in_hbm, step_in),
+    ]
+    loads = [
+        pltpu.make_async_copy(source, target, in_sems.at[number])
+        for number, (source, target) in enumerate(held)
+    ]
+    for load in loads:
+        load.start()
 
     x_first[...] = jnp.zeros_like(x_first)
     x_got[...] = jnp.zeros_like(x_got)
@@ -269,6 +301,8 @@
     lane16, row16 = lane[:16], row[:16]
     r16 = jnp.where(lane16 < ELEMS, lane16 % EZ, EZ)
 
+    for load in loads[:3]:
+        load.wait()
     flat[0:3, :] = disp_in[...]
     flat[3:6, :] = vel_in[...]
     stacked = jnp.concatenate([flat[:, plane * x : plane * (x + 1)] for x in range(3)], axis=0)
@@ -385,6 +419,8 @@
 
     started = exchange_start(0, first, 6, lambda slot: x_first, True, False)
 
+    for load in loads[3:]:
+        load.wait()
     step = step_in[0, 0]
     density_pad[0:ELEMS, 0:125] = density_in[...]
     energy_pad[0:27, 0:ELEMS] = energy_in[...]
@@ -663,25 +699,30 @@
 
 
 def hand_on(*refs):
-    for source, target in zip(refs[:3], refs[3:]):
-        target[...] = source[...]
+    copies = [
+        pltpu.make_async_copy(refs[k], refs[3 + k], refs[6].at[k]) for k in range(3)
+    ]
+    for copy in copies:
+        copy.start()
+    for copy in copies:
+        copy.wait()
 
 
 def body(n_dom, n_sub, displacement, velocity, energy, mass_density, live_mask, time_step):
     forward, backward, energy_pair, quad_weight, pick = tables()
     vmem = pl.BlockSpec(memory_space=pltpu.VMEM)
-    smem = pl.BlockSpec(memory_space=pltpu.SMEM)
+    anywhere = pl.BlockSpec(memory_space=pl.ANY)
     f32 = jnp.float32
     nodes = displacement.shape[1]
     wide_sum = n_dom * n_sub if n_dom * n_sub <= 64 else n_dom
     made = pl.pallas_call(
         functools.partial(kernel, n_dom, n_sub),
         out_shape=(
-            jax.ShapeDtypeStruct(displacement.shape, f32),
-            jax.ShapeDtypeStruct(energy.shape, f32),
-            jax.ShapeDtypeStruct(displacement.shape, f32),
+            pltpu.VMEM(displacement.shape, f32),
+            pltpu.VMEM(energy.shape, f32),
+            pltpu.VMEM(displacement.shape, f32),
         ),
-        in_specs=[vmem] * 5 + [smem] + [vmem] * 5,
+        in_specs=[anywhere] * 11,
         out_specs=(vmem, vmem, vmem),
         scratch_shapes=[
             pltpu.VMEM((8, nodes), f32),
@@ -707,6 +748,18 @@
             pltpu.SemaphoreType.DMA((wide_sum,)),
             pltpu.SemaphoreType.DMA((n_sub,)),
             pltpu.SemaphoreType.DMA((n_sub,)),
+            pltpu.VMEM(displacement.shape, f32),
+            pltpu.VMEM(velocity.shape, f32),
+            pltpu.VMEM(energy.shape, f32),
+            pltpu.VMEM(mass_density.shape[::-1], f32),
+            pltpu.VMEM((1, live_mask.shape[0]), jnp.int32),
+            pltpu.SMEM((1, 1), f32),
+            pltpu.VMEM(forward.shape, f32),
+            pltpu.VMEM(backward.shape, f32),
+            pltpu.VMEM(energy_pair.shape, f32),
+            pltpu.VMEM(quad_weight.shape, f32),
+            pltpu.VMEM(pick.shape, jnp.bfloat16),
+            pltpu.SemaphoreType.DMA((11,)),
         ],
         compiler_params=pltpu.CompilerParams(collective_id=0, has_side_effects=True),
     )(
@@ -726,8 +779,9 @@
         hand_on,
         out_shape=[jax.ShapeDtypeStruct(m.shape, f32) for m in made],
         in_specs=[vmem] * 3,
-        out_specs=[vmem] * 3,
-    )(*made)
+        out_specs=[anywhere] * 3,
+        scratch_shapes=[pltpu.SemaphoreType.DMA((3,))],
+    )(*[pltpu.with_memory_space_constraint(m, pltpu.VMEM) for m in made])
 
 
 def solution(mesh):

time: 38.1 us -> 35.3 us (0.927)
  Pallas kernels: 36.5 us -> 33.7 us
    pallas_call x1, Pallas kernels: 35.1 us -> 33.1 us  [body(): pl.pallas_call(functools.partial(kernel, n_dom, n_sub), out_shape=(pltpu....]
    pallas_call x1, Pallas kernels: 1.4 us -> 0.65 us  [body(): pl.pallas_call(hand_on, out_shape=[jax.ShapeDtypeStruct(m.shape, f32) for...]
where the time goes in v1:
time: 35.3 us; the launch traced here: 35 us
  Pallas kernels  33.7 us (95%)
  between operations  1.29 us (4%)
    pallas_call x1, Pallas kernels, body(): pl.pallas_call(functools.partial(kernel, n_dom, n_sub), out_shape=(pltpu....  33.1 us

profile of v1, /device:TPU:0, one launch (start us, length us, event | category | flops | bytes accessed | tf_op | source)
XLA Modules:
  0.0 35.0 jit_solution(4298363084003667907)
XLA Ops:
  1.3 33.1 %shard_map.130 = (f32[3,1350]{1,0:T(4,128)S(1)}, f32[27,48]{1,0:T(8,128)S(1)}, f32[3,1350]{1,0:T(4,128)S(1)}) custom-call(f32[3,1350]{1,0:T(4,128)} %disp_in_hbm.1, f32[3,1350]{1,0:T(4,128)} %vel_in_hbm.1, f32[27,48]{1,0:T(8,128)} %energy_in_hbm.1, f32[48,125]{1,0:T(8,128)} %bitcast.4, s32[1,48]{1,0:T(1,128)} %bitcast.5, f32[1,1]{1,0:T(1,128)} %bitcast.3.step_in_hbm, ...), custom_call_target="tpu_custom_call" | custom-call | tf_op jit(solution)/shard_map/pallas_call | solution.py:718
  34.4 0.6 %shard_map.131 = (f32[3,1350]{1,0:T(4,128)}, f32[27,48]{1,0:T(8,128)}, f32[3,1350]{1,0:T(4,128)}) custom-call(f32[3,1350]{1,0:T(4,128)S(1)} %get-tuple-element.6.refs_0_, f32[27,48]{1,0:T(8,128)S(1)} %get-tuple-element.7.refs_1_, f32[3,1350]{1,0:T(4,128)S(1)} %get-tuple-element.8.refs_2_), custom_call_target="tpu_custom_call" | custom-call | tf_op jit(solution)/shard_map/pallas_call | solution.py:778

commit v2 on v1

--- a/solution.py
+++ b/solution.py
@@ -14,12 +14,14 @@
 EZ = 6
 ELEMS = EX * EY * EZ
 HALF = 64
+ROW = 8
 
 adiabatic = 5.0 / 3.0
 viscosity = 0.3
 mesh_step = 0.01
 MESH = pl.DeviceIdType.MESH
 STEPS = [(dx, dz) for dx in (-1, 0, 1) for dz in (-1, 0, 1) if (dx, dz) != (0, 0)]
+WIDE_STEPS = [(dx, dz) for dx in (-2, -1, 0, 1) for dz in (-1, 0, 1) if (dx, dz) != (0, 0)]
 
 
 def one_dimension():
@@ -60,29 +62,31 @@
     return np.concatenate([padded[:64], padded[64:]], axis=1)
 
 
+def stacked_left(table):
+    table = np.asarray(table, np.float32)
+    high = table.astype(jnp.bfloat16)
+    low = (table - high.astype(np.float32)).astype(jnp.bfloat16)
+    return np.concatenate([low, high, high], axis=1)
+
+
 @functools.lru_cache(None)
 def tables():
     values, slopes, bernstein, weights = one_dimension()
+    triples = [
+        outer_triple(slopes, values, values),
+        outer_triple(values, slopes, values),
+        outer_triple(values, values, slopes),
+    ]
+    grad = np.concatenate([halves(t, 64) for t in triples], axis=0)
+    whole = [np.concatenate([t, np.repeat(t[-1:], 3, axis=0)], axis=0) for t in triples]
     basis = halves(outer_triple(values, values, values), 64)
-    grad = np.concatenate(
-        [
-            halves(outer_triple(slopes, values, values), 64),
-            halves(outer_triple(values, slopes, values), 64),
-            halves(outer_triple(values, values, slopes), 64),
-        ],
-        axis=0,
-    )
     energy = halves(outer_triple(bernstein, bernstein, bernstein), 32)
-    forward = np.concatenate([grad, basis], axis=0)
-    backward = np.zeros((128, 384))
-    backward[:, :192] = grad.T
-    backward[:, 256:320] = basis.T
-    energy_pair = np.concatenate([energy, energy.T], axis=1)
     weight = np.einsum("i,j,k->ijk", weights, weights, weights).reshape(125)
     weight = np.pad(weight, (0, 3))
     spread_weight = np.zeros((64, 128))
-    spread_weight[:, :ELEMS] = weight[:64, None]
-    spread_weight[:, 64 : 64 + ELEMS] = weight[64:, None]
+    spread_weight[:, :64] = weight[:64, None]
+    spread_weight[:, 64:] = weight[64:, None]
+    whole_weight = np.repeat(weight[:, None], 128, axis=1)
     planes_y, planes_z = 3 * EY + 1, 3 * EZ
     pick = np.zeros((planes_y * planes_z, 16 * HALF), np.float32)
     for b in range(4):
@@ -91,20 +95,33 @@
                 for r in range(EZ):
                     z = 3 * r + c - 1
                     if z >= 0:
-                        lane = (4 * b + c) * HALF + q * EZ + r
+                        lane = (4 * b + c) * HALF + q * ROW + r
                         pick[(3 * q + b) * planes_z + z, lane] = 1.0
-    return [np.asarray(t, np.float32) for t in (forward, backward, energy_pair, spread_weight)] + [
-        pick
+    widen = np.zeros((128, 256), np.float32)
+    for e in range(ELEMS):
+        to = e // EZ * ROW + e % EZ
+        widen[e, to] = 1.0
+        widen[to, 128 + e] = 1.0
+    return [
+        pick.astype(jnp.bfloat16),
+        stacked_left(grad),
+        stacked_left(grad.T),
+        stacked_left(basis),
+        stacked_left(basis.T),
+        stacked_left(energy),
+        stacked_left(energy.T),
+        stacked_left(np.concatenate(whole, axis=0)),
+        stacked_left(np.concatenate(whole, axis=0).T),
+        widen.astype(jnp.bfloat16),
+        np.asarray(spread_weight, np.float32),
+        np.asarray(whole_weight, np.float32),
     ]
 
 
-def dot(left, right):
-    left_high, left_low = split_two(left)
-    right_high, right_low = split_two(right)
-    product = functools.partial(jnp.dot, preferred_element_type=jnp.float32)
-    return (
-        product(left_low, right_high) + product(left_high, right_low)
-    ) + product(left_high, right_high)
+def dot(table, right):
+    high, low = split_two(right)
+    stacked = jnp.concatenate([high, low, high], axis=0)
+    return jnp.dot(table[...], stacked, preferred_element_type=jnp.float32)
 
 
 def split_two(value):
@@ -147,11 +164,18 @@
     density_in_hbm,
     live_in_hbm,
     step_in_hbm,
-    forward_hbm,
-    backward_hbm,
-    energy_pair_hbm,
+    pick_hbm,
+    grad_forth_hbm,
+    grad_back_hbm,
+    basis_forth_hbm,
+    basis_back_hbm,
+    energy_forth_hbm,
+    energy_back_hbm,
+    whole_forth_hbm,
+    whole_back_hbm,
+    widen_hbm,
     quad_weight_hbm,
-    pick_hbm,
+    whole_weight_hbm,
     new_vel_out,
     rate_out,
     mesh_vel_out,
@@ -164,7 +188,8 @@
     out_wide,
     density_pad,
     energy_pad,
-    live_pad,
+    live_own,
+    live_got,
     packs,
     x_first,
     x_got,
@@ -184,12 +209,33 @@
     density_in,
     live_in,
     step_in,
-    forward,
-    backward,
-    energy_pair,
+    pick,
+    grad_forth,
+    grad_back,
+    basis_forth,
+    basis_back,
+    energy_forth,
+    energy_back,
+    whole_forth,
+    whole_back,
+    widen,
     quad_weight,
-    pick,
+    whole_weight,
     in_sems,
+    ours,
+    near,
+    z_low,
+    z_high,
+    slab_got,
+    x_face_got,
+    layer_got,
+    edge_got,
+    floor_got,
+    wide_nodes,
+    wide_send,
+    wide_recv,
+    live_send,
+    live_recv,
 ):
     dom = lax.axis_index("dom")
     sub = lax.axis_index("sub")
@@ -199,7 +245,7 @@
         ok = None
         for step, place, size in ((dx, dom, n_dom), (dz, sub, n_sub)):
             if step:
-                here = (place > 0) if step < 0 else (place < size - 1)
+                here = (place + step >= 0) if step < 0 else (place + step < size)
                 ok = here if ok is None else jnp.logical_and(ok, here)
         return ok
 
@@ -207,14 +253,21 @@
         (disp_in_hbm, disp_in),
         (vel_in_hbm, vel_in),
         (pick_hbm, pick),
-        (forward_hbm, forward),
-        (backward_hbm, backward),
+        (step_in_hbm, step_in),
         (density_in_hbm, density_in),
         (energy_in_hbm, energy_in),
         (live_in_hbm, live_in),
-        (energy_pair_hbm, energy_pair),
+        (grad_forth_hbm, grad_forth),
+        (grad_back_hbm, grad_back),
+        (basis_forth_hbm, basis_forth),
+        (basis_back_hbm, basis_back),
+        (energy_forth_hbm, energy_forth),
+        (energy_back_hbm, energy_back),
+        (whole_forth_hbm, whole_forth),
+        (whole_back_hbm, whole_back),
+        (widen_hbm, widen),
         (quad_weight_hbm, quad_weight),
-        (step_in_hbm, step_in),
+        (whole_weight_hbm, whole_weight),
     ]
     loads = [
         pltpu.make_async_copy(source, target, in_sems.at[number])
@@ -227,6 +280,8 @@
     x_got[...] = jnp.zeros_like(x_got)
     z_got[...] = jnp.zeros_like(z_got)
     d_got[...] = jnp.zeros_like(d_got)
+    for got in (slab_got, x_face_got, layer_got, edge_got, floor_got, live_got):
+        got[...] = jnp.zeros_like(got)
 
     barrier = pltpu.get_barrier_semaphore()
     one_phase = n_dom * n_sub <= 64
@@ -246,7 +301,7 @@
 
     else:
         count = (n_dom - 1) + (n_sub - 1)
-        for dx, dz in STEPS:
+        for dx, dz in [(dx, dz) for dx in (-2, -1, 1, 2) for dz in (-1, 1)]:
             if dx and dz:
                 ok = inside(dx, dz)
                 count = count + ok.astype(jnp.int32)
@@ -272,15 +327,15 @@
     first[...] = jnp.zeros_like(first)
     density_pad[...] = jnp.zeros_like(density_pad)
     energy_pad[...] = jnp.zeros_like(energy_pad)
-    live_pad[...] = jnp.zeros_like(live_pad)
     flat[...] = jnp.zeros_like(flat)
     out_wide[...] = jnp.zeros_like(out_wide)
 
     lane = lax.broadcasted_iota(jnp.int32, (64, 128), 1)
     row = lax.broadcasted_iota(jnp.int32, (64, 128), 0)
-    q_of, r_of = lane // EZ, lane % EZ
+    q_of, r_of = (lane % HALF) // ROW, lane % ROW
     a_of, b_of, c_of = row // 16, (row // 4) % 4, row % 4
-    valid = lane < ELEMS
+    low_half = lane < HALF
+    valid = low_half & (r_of < EZ)
     triple = lambda x: jnp.concatenate([x, x, x], axis=0)
     y_up = triple((b_of == 3) & (q_of < EY - 1) & valid)
     y_down = triple((b_of == 0) & (q_of > 0) & valid)
@@ -299,7 +354,7 @@
     )
     owned = triple(owned)
     lane16, row16 = lane[:16], row[:16]
-    r16 = jnp.where(lane16 < ELEMS, lane16 % EZ, EZ)
+    r16 = jnp.where(lane16 < HALF, lane16 % ROW, ROW)
 
     for load in loads[:3]:
         load.wait()
@@ -422,20 +477,42 @@
     for load in loads[3:]:
         load.wait()
     step = step_in[0, 0]
-    density_pad[0:ELEMS, 0:125] = density_in[...]
+    for q in range(EY):
+        density_pad[ROW * q : ROW * q + EZ, 0:125] = density_in[EZ * q : EZ * q + EZ, :]
     energy_pad[0:27, 0:ELEMS] = energy_in[...]
-    live_pad[0:1, 0:ELEMS] = live_in[...].astype(jnp.float32)
-    live = live_pad[0:1, :]
+    energy_pad[27:28, 0:ELEMS] = live_in[...].astype(jnp.float32)
+
+    def exact(value, table):
+        rows = value.shape[0]
+        out = jnp.dot(split_three(value), table, preferred_element_type=jnp.float32)
+        return out[0:rows] + out[rows : 2 * rows] + out[2 * rows :]
+
+    by_lane = exact(energy_pad[...], widen[:, 0:128])
+    live = by_lane[27:28, :]
+    live_own[...] = jnp.broadcast_to(live, (8, 128))
+    live_copies = []
+    for number, (dx, dz) in enumerate(((-1, 0), (0, -1), (-1, -1))):
+        live_copy = pltpu.make_async_remote_copy(
+            src_ref=live_own,
+            dst_ref=live_got.at[number],
+            send_sem=live_send.at[number],
+            recv_sem=live_recv.at[number],
+            device_id=(dom + dx, sub + dz),
+            device_id_type=MESH,
+        )
+        live_copies.append((live_copy, (dx, dz)))
+
+        @pl.when(inside(dx, dz))
+        def _():
+            live_copy.start()
+
     live = live + turn(live, 0, 64)
     by_point = jnp.transpose(density_pad[...])
     mass_density = by_point[0:64] + turn(by_point[64:128], 0, 64)
     weight = quad_weight[...]
     live_weight = weight * live
     mass_weight = live_weight * mass_density
-    energy_pad_v = energy_pad[...]
-    at_points = dot(
-        energy_pair[:, 0:64], jnp.concatenate([energy_pad_v, turn(energy_pad_v, 0, 64)], axis=0)
-    )
+    at_points = dot(energy_forth, jnp.concatenate([by_lane, turn(by_lane, 0, 64)], axis=0))
 
     def paired(v):
         return jnp.concatenate(
@@ -455,7 +532,7 @@
         return out
 
     def gradient(v):
-        shaped = dot(forward[0:192, :], paired(v))
+        shaped = dot(grad_forth, paired(v))
         return [
             [shaped[64 * m : 64 * m + 64, 128 * c : 128 * c + 128] for m in range(3)]
             for c in range(3)
@@ -471,16 +548,16 @@
         right = jnp.concatenate(
             [jnp.concatenate([fields[c][m] for c in range(3)], axis=1) for m in range(3)], axis=0
         )
-        return share(jnp.concatenate(folded(dot(backward[:, 0:192], right)), axis=0))
+        return share(jnp.concatenate(folded(dot(grad_back, right)), axis=0))
 
     def share(v):
         v = v * jnp.where(triple(valid), 1.0, 0.0)
-        v = v + jnp.where(y_up, turn(v, 12, -EZ), 0.0) + jnp.where(y_down, turn(v, -12, EZ), 0.0)
+        v = v + jnp.where(y_up, turn(v, 12, -ROW), 0.0) + jnp.where(y_down, turn(v, -12, ROW), 0.0)
         v = v + jnp.where(z_up, turn(v, 3, -1), 0.0) + jnp.where(z_down, turn(v, -3, 1), 0.0)
         return v
 
     def interpolate(v):
-        return dot(forward[192:256, :], paired(v))
+        return dot(basis_forth, paired(v))
 
     def volume_of(jacobian, cofactor):
         return (
@@ -553,15 +630,16 @@
                 power = power + stress[c][m] * spatial[c][m]
     power = live_weight * volume * power
     sums = folded(
-        dot(energy_pair[:, 64:128], jnp.concatenate([power, weight * mass_density], axis=1))
-    )
-    rate_out[...] = (sums[0] / sums[1])[0:27, 0:ELEMS]
+        dot(energy_back, jnp.concatenate([power, weight * mass_density], axis=1))
+    )
+    rates = jnp.where(valid[:32], sums[0] / jnp.where(valid[:32], sums[1], 1.0), 0.0)
+    rate_out[...] = exact(rates, widen[:, 128:256])[0:27, 0:ELEMS]
     force = finish(1, started)
 
     wide_mass = jnp.concatenate([mass_weight] * 3, axis=1)
     values = interpolate(force)
     weighted = wide_mass * values
-    image = share(jnp.concatenate(folded(dot(backward[:, 256:320], weighted)), axis=0))
+    image = share(jnp.concatenate(folded(dot(basis_back, weighted)), axis=0))
     started = begin(2, image)
 
     def total(x):
@@ -587,7 +665,7 @@
 
     late = []
 
-    def all_sum(value, slots, size, place, target, sends, recvs):
+    def all_sum(value, slots, size, place, target, sends, recvs, cover=None):
         slots[0] = value
 
         def copy_of(i):
@@ -604,17 +682,20 @@
         def _(i):
             copy_of(i).start()
 
+        out = cover() if cover else None
+
         @pl.loop(1, size, unroll=True)
         def _(i):
             copy_of(i).wait_recv()
 
-        out = jnp.sum(slots[...], axis=0)
-
         late.append((copy_of, size))
-        return out
+        return jnp.sum(slots[...], axis=0), out
+
+    def ahead():
+        return [gradient(v) for v in (displacement + step * velocity, force, image)]
 
     if one_phase:
-        packed = all_sum(
+        packed, slopes = all_sum(
             packed,
             sum_dom,
             n_dom * n_sub,
@@ -622,10 +703,13 @@
             lambda t: (t // n_sub, lax.rem(t, n_sub)),
             dom_send,
             dom_recv,
+            ahead,
         )
     else:
-        packed = all_sum(packed, sum_dom, n_dom, dom, lambda t: (t, sub), dom_send, dom_recv)
-        packed = all_sum(packed, sum_sub, n_sub, sub, lambda t: (dom, t), sub_send, sub_recv)
+        packed, slopes = all_sum(
+            packed, sum_dom, n_dom, dom, lambda t: (t, sub), dom_send, dom_recv, ahead
+        )
+        packed, _ = all_sum(packed, sum_sub, n_sub, sub, lambda t: (dom, t), sub_send, sub_recv)
     rr, rw, ww, wmw = (
         jnp.sum(jnp.where(lane1 == k, packed, 0.0), axis=1, keepdims=True) for k in range(4)
     )
@@ -641,8 +725,7 @@
     new_velocity = velocity + step * (on_force * force - on_image * image)
     moved = displacement + step * new_velocity
 
-    def shape(v):
-        jacobian = jacobian_of(v)
+    def fluxes(jacobian, weights):
         cofactor = cofactors(jacobian)
         volume = volume_of(jacobian, cofactor)
         norm_sq = None
@@ -650,21 +733,159 @@
             for m in range(3):
                 square = jacobian[c][m] * jacobian[c][m]
                 norm_sq = square if norm_sq is None else norm_sq + square
-        scale = live_weight * jnp.exp(jnp.log(volume) * (-2.0 / 3.0))
+        scale = weights * jnp.exp(jnp.log(volume) * (-2.0 / 3.0))
         along = scale * (2.0 / 3.0)
         across = scale * (2.0 / 9.0) * (norm_sq / volume)
-        return project(
-            [
-                [along * jacobian[c][m] - across * cofactor[c][m] for m in range(3)]
-                for c in range(3)
-            ]
+        return [
+            [along * jacobian[c][m] - across * cofactor[c][m] for m in range(3)]
+            for c in range(3)
+        ]
+
+    by_force, by_image = step * step * on_force, step * step * on_image
+    jacobian = [
+        [
+            slopes[0][c][m] + by_force * slopes[1][c][m] - by_image * slopes[2][c][m]
+            for m in range(3)
+        ]
+        for c in range(3)
+    ]
+    for c in range(3):
+        jacobian[c][c] = jacobian[c][c] + 1.0
+    shift = -mesh_step * project(fluxes(jacobian, live_weight))
+
+    comps = range(3)
+    a_first, c_first = a_of == 0, c_of == 0
+    part = [shift[64 * k : 64 * k + 64] for k in comps]
+    whole = [moved[64 * k : 64 * k + 64] + part[k] for k in comps]
+    ours[...] = shift
+    slab = jnp.concatenate([jnp.where(a_first, part[k], whole[k]) for k in comps], axis=0)
+    near[...] = slab[0:96] + turn(slab[96:192], 0, 64)
+    r64 = jnp.where(low_half, r_of, ROW)
+
+    def lay(fields, place):
+        out = None
+        for k in comps:
+            at = r64[: fields[k].shape[0]]
+            piece = jnp.where(at == k, turn(fields[k], 0, k - place), 0.0)
+            out = piece if out is None else out + piece
+        return out + turn(out, 0, 64)
+
+    layer = lay([jnp.where(c_first, part[k], whole[k]) for k in comps], 0)
+    z_low[0:16] = lay([part[k][0:16] for k in comps], 0)
+    z_low[16:64] = layer[16:64]
+    z_low[64:80] = layer[0:16]
+    z_low[80:96] = lay([part[k][48:64] for k in comps], 0)
+    z_high[...] = lay([ours[pl.ds(64 * k + 3, 16, stride=4), :] for k in comps], EZ - 1)
+
+    blocks = ours.reshape(3, 64, 128)
+    routes = {
+        (-1, 0): (near, slab_got),
+        (-2, 0): (blocks.at[:, pl.ds(0, 16)], x_face_got.at[0]),
+        (1, 0): (blocks.at[:, pl.ds(48, 16)], x_face_got.at[1]),
+        (0, -1): (z_low.at[pl.ds(16, 64)], layer_got.at[0]),
+        (-1, -1): (z_low.at[pl.ds(0, 64)], layer_got.at[1]),
+        (-2, -1): (z_low.at[pl.ds(0, 16)], edge_got.at[0]),
+        (1, -1): (z_low.at[pl.ds(80, 16)], edge_got.at[1]),
+        (0, 1): (z_high, floor_got.at[0]),
+        (-1, 1): (z_high, floor_got.at[1]),
+        (-2, 1): (z_high, floor_got.at[2]),
+        (1, 1): (z_high, floor_got.at[3]),
+    }
+    started = []
+    for number, (dx, dz) in enumerate(WIDE_STEPS):
+        source, target = routes[dx, dz]
+        wide_copy = pltpu.make_async_remote_copy(
+            src_ref=source,
+            dst_ref=target,
+            send_sem=wide_send.at[number],
+            recv_sem=wide_recv.at[number],
+            device_id=(dom + dx, sub + dz),
+            device_id_type=MESH,
         )
 
-    started = begin(3, shape(moved))
-    slope = finish(3, started)
-    started = begin(4, shape(moved - mesh_step * slope), False, True)
-    last = finish(4, started, False, True)
-    mesh_velocity = new_velocity - (mesh_step / step) * (slope + last)
+        @pl.when(inside(dx, dz))
+        def _():
+            wide_copy.start()
+
+        started.append((wide_copy, (dx, dz)))
+    exchange_wait(live_copies)
+    high_half = jnp.logical_not(low_half)
+    one_low, one_r = low_half[0:1], r_of[0:1]
+    live_up = turn(live_got[0, 0:1, :], 0, 64)
+    live_layer = live_got[1, 0:1, :] + turn(live_got[2, 0:1, :], 0, 64)
+    live_wide = live_own[0:1, :] + live_up + jnp.where(one_r == EZ, turn(live_layer, 0, EZ), 0.0)
+    wide_weight = whole_weight[...] * live_wide
+    wide_wall = jnp.where(
+        jnp.logical_or(high_half, jnp.logical_or(a_of > 0, dom > 0))
+        & jnp.logical_or(jnp.logical_or(c_of > 0, r_of > 0), sub > 0),
+        1.0,
+        0.0,
+    )
+    low16, row16r = low_half[:16], r_of[:16]
+
+    exchange_wait(started)
+    upper = slab_got[...]
+    upper = jnp.concatenate([turn(upper, 0, 64), upper], axis=0)
+    layers = jnp.where(
+        low_half,
+        jnp.concatenate([layer_got[0, 48:64], layer_got[0, 0:48]], axis=0),
+        layer_got[1],
+    )
+    layers = layers + jnp.concatenate(
+        [
+            jnp.where(low16, edge_got[1], 0.0),
+            jnp.zeros((32, 128), jnp.float32),
+            jnp.where(low16, 0.0, edge_got[0]),
+        ],
+        axis=0,
+    )
+    floor = jnp.where(low16, floor_got[0], floor_got[1])
+    floor = floor + jnp.where(jnp.logical_not(low16) & (row16 >= 12), turn(floor_got[2], 12, 0), 0.0)
+    floor = floor + jnp.where(low16 & (row16 < 4), turn(floor_got[3], 4, 0), 0.0)
+    for k in comps:
+        at = 64 * k
+        u = jnp.where(low_half, whole[k], upper[at : at + 64])
+        u = u + jnp.where(r_of == EZ, turn(layers, 0, EZ - k), 0.0)
+        wide_nodes[at : at + 64, :] = u
+        wide_nodes[at : at + 16, :] += x_face_got[1, k]
+        wide_nodes[at + 48 : at + 64, :] += turn(x_face_got[0, k], 0, 64)
+        below = pl.ds(at, 16, stride=4)
+        above = pl.ds(at + 3, 16, stride=4)
+        wide_nodes[below, :] += jnp.where(row16r == 0, turn(floor, 0, -k), 0.0)
+        wide_nodes[at + 48 : at + 64, :] += jnp.where(
+            low16, turn(wide_nodes[at : at + 16, :], 0, 64), 0.0
+        )
+        tops = wide_nodes[above, :]
+        bottoms = wide_nodes[below, :]
+        tops = tops + jnp.where(row16r == EZ - 1, turn(bottoms, 0, -1), 0.0)
+        wide_nodes[above, :] = tops
+        wide_nodes[below, :] = jnp.where(row16r == EZ, turn(tops, 0, 1), bottoms)
+        wide_nodes[at : at + 16, :] = jnp.where(
+            low16,
+            wide_nodes[at : at + 16, :],
+            turn(wide_nodes[at + 48 : at + 64, :], 0, 64),
+        )
+    relaxed = [wide_nodes[64 * k : 64 * k + 64, :] * wide_wall for k in comps]
+    shaped = dot(whole_forth, jnp.concatenate(relaxed, axis=1))
+    jacobian = [
+        [shaped[128 * m : 128 * m + 128, 128 * c : 128 * c + 128] for m in comps] for c in comps
+    ]
+    for c in comps:
+        jacobian[c][c] = jacobian[c][c] + 1.0
+    fields = fluxes(jacobian, wide_weight)
+    right = jnp.concatenate(
+        [jnp.concatenate([fields[c][m] for c in comps], axis=1) for m in comps], axis=0
+    )
+    product = dot(whole_back, right)
+    last = []
+    for k in comps:
+        v = product[:, 128 * k : 128 * k + 128]
+        v = v + jnp.where((b_of == 0) & (q_of > 0), turn(v, -12, ROW), 0.0)
+        v = v + jnp.where((c_of == 3) & (r_of < EZ), turn(v, 3, -1), 0.0)
+        v = jnp.concatenate([v[0:48], v[48:64] + turn(v[0:16], 0, 64)], axis=0)
+        last.append(moved[64 * k : 64 * k + 64] - relaxed[k] + mesh_step * v)
+    last = jnp.concatenate(last, axis=0)
+    mesh_velocity = new_velocity - last / step
 
     out_nodes[0:192, :] = new_velocity * owned
     out_nodes[192:384, :] = mesh_velocity * owned
@@ -709,7 +930,7 @@
 
 
 def body(n_dom, n_sub, displacement, velocity, energy, mass_density, live_mask, time_step):
-    forward, backward, energy_pair, quad_weight, pick = tables()
+    made_tables = tables()
     vmem = pl.BlockSpec(memory_space=pltpu.VMEM)
     anywhere = pl.BlockSpec(memory_space=pl.ANY)
     f32 = jnp.float32
@@ -722,28 +943,29 @@
             pltpu.VMEM(energy.shape, f32),
             pltpu.VMEM(displacement.shape, f32),
         ),
-        in_specs=[anywhere] * 11,
+        in_specs=[anywhere] * (6 + len(made_tables)),
         out_specs=(vmem, vmem, vmem),
         scratch_shapes=[
             pltpu.VMEM((8, nodes), f32),
             pltpu.VMEM((24, 1024), f32),
             pltpu.VMEM((512, 128), f32),
-            pltpu.VMEM((4, 192, 128), f32),
+            pltpu.VMEM((2, 192, 128), f32),
             pltpu.VMEM((192, 128), f32),
             pltpu.VMEM((384, 128), f32),
             pltpu.VMEM((24, 1024), f32),
             pltpu.VMEM((128, 128), f32),
             pltpu.VMEM((32, 128), f32),
             pltpu.VMEM((8, 128), f32),
-            pltpu.VMEM((5, 2, 16, 128), f32),
+            pltpu.VMEM((3, 8, 128), f32),
+            pltpu.VMEM((3, 2, 16, 128), f32),
             pltpu.VMEM((6, 16, 128), f32),
-            pltpu.VMEM((4, 2, 3, 16, 128), f32),
-            pltpu.VMEM((5, 2, 16, 128), f32),
-            pltpu.VMEM((5, 4, 8, 128), f32),
+            pltpu.VMEM((2, 2, 3, 16, 128), f32),
+            pltpu.VMEM((3, 2, 16, 128), f32),
+            pltpu.VMEM((3, 4, 8, 128), f32),
             pltpu.VMEM((wide_sum, 1, 128), f32),
             pltpu.VMEM((n_sub, 1, 128), f32),
-            pltpu.SemaphoreType.DMA((5, 8)),
-            pltpu.SemaphoreType.DMA((5, 8)),
+            pltpu.SemaphoreType.DMA((3, 8)),
+            pltpu.SemaphoreType.DMA((3, 8)),
             pltpu.SemaphoreType.DMA((wide_sum,)),
             pltpu.SemaphoreType.DMA((wide_sum,)),
             pltpu.SemaphoreType.DMA((n_sub,)),
@@ -754,12 +976,22 @@
             pltpu.VMEM(mass_density.shape[::-1], f32),
             pltpu.VMEM((1, live_mask.shape[0]), jnp.int32),
             pltpu.SMEM((1, 1), f32),
-            pltpu.VMEM(forward.shape, f32),
-            pltpu.VMEM(backward.shape, f32),
-            pltpu.VMEM(energy_pair.shape, f32),
-            pltpu.VMEM(quad_weight.shape, f32),
-            pltpu.VMEM(pick.shape, jnp.bfloat16),
-            pltpu.SemaphoreType.DMA((11,)),
+            *[pltpu.VMEM(t.shape, t.dtype) for t in made_tables],
+            pltpu.SemaphoreType.DMA((6 + len(made_tables),)),
+            pltpu.VMEM((192, 128), f32),
+            pltpu.VMEM((96, 128), f32),
+            pltpu.VMEM((96, 128), f32),
+            pltpu.VMEM((16, 128), f32),
+            pltpu.VMEM((96, 128), f32),
+            pltpu.VMEM((2, 3, 16, 128), f32),
+            pltpu.VMEM((2, 64, 128), f32),
+            pltpu.VMEM((2, 16, 128), f32),
+            pltpu.VMEM((4, 16, 128), f32),
+            pltpu.VMEM((192, 128), f32),
+            pltpu.SemaphoreType.DMA((len(WIDE_STEPS),)),
+            pltpu.SemaphoreType.DMA((len(WIDE_STEPS),)),
+            pltpu.SemaphoreType.DMA((3,)),
+            pltpu.SemaphoreType.DMA((3,)),
         ],
         compiler_params=pltpu.CompilerParams(collective_id=0, has_side_effects=True),
     )(
@@ -769,11 +1001,7 @@
         mass_density.T,
         live_mask.reshape(1, -1),
         time_step.reshape(1, 1),
-        forward,
-        backward,
-        energy_pair,
-        quad_weight,
-        jnp.asarray(pick, jnp.bfloat16),
+        *[jnp.asarray(t) for t in made_tables],
     )
     return pl.pallas_call(
         hand_on,

time: 35.3 us -> 33 us (0.935)
  Pallas kernels: 33.7 us -> 31.6 us
    pallas_call x1, Pallas kernels: 33.1 us -> 30.9 us  [body(): pl.pallas_call(functools.partial(kernel, n_dom, n_sub), out_shape=(pltpu....]
where the time goes in v2:
time: 33 us; the launch traced here: 32.9 us
  Pallas kernels  31.6 us (96%)
  between operations  1.29 us (4%)
    pallas_call x1, Pallas kernels, body(): pl.pallas_call(functools.partial(kernel, n_dom, n_sub), out_shape=(pltpu....  30.9 us

profile of v2, /device:TPU:0, one launch (start us, length us, event | category | flops | bytes accessed | tf_op | source)
XLA Modules:
  0.0 32.9 jit_solution(17994456420602586044)
XLA Ops:
  1.3 30.9 %shard_map.193 = (f32[3,1350]{1,0:T(4,128)S(1)}, f32[27,48]{1,0:T(8,128)S(1)}, f32[3,1350]{1,0:T(4,128)S(1)}) custom-call(f32[3,1350]{1,0:T(4,128)} %disp_in_hbm.1, f32[3,1350]{1,0:T(4,128)} %vel_in_hbm.1, f32[27,48]{1,0:T(8,128)} %energy_in_hbm.1, f32[48,125]{1,0:T(8,128)} %bitcast.4, s32[1,48]{1,0:T(1,128)} %bitcast.5, f32[1,1]{1,0:T(1,128)} %bitcast.3.step_in_hbm, ...), custom_call_target="tpu_custom_call" | custom-call | tf_op jit(solution)/shard_map/pallas_call | solution.py:939
  32.2 0.6 %shard_map.194 = (f32[3,1350]{1,0:T(4,128)}, f32[27,48]{1,0:T(8,128)}, f32[3,1350]{1,0:T(4,128)}) custom-call(f32[3,1350]{1,0:T(4,128)S(1)} %get-tuple-element.6.refs_0_, f32[27,48]{1,0:T(8,128)S(1)} %get-tuple-element.7.refs_1_, f32[3,1350]{1,0:T(4,128)S(1)} %get-tuple-element.8.refs_2_), custom_call_target="tpu_custom_call" | custom-call | tf_op jit(solution)/shard_map/pallas_call | solution.py:1006

commit v3 on v2

--- a/solution.py
+++ b/solution.py
@@ -21,7 +21,8 @@
 mesh_step = 0.01
 MESH = pl.DeviceIdType.MESH
 STEPS = [(dx, dz) for dx in (-1, 0, 1) for dz in (-1, 0, 1) if (dx, dz) != (0, 0)]
-WIDE_STEPS = [(dx, dz) for dx in (-2, -1, 0, 1) for dz in (-1, 0, 1) if (dx, dz) != (0, 0)]
+WIDE_STEPS = [(-2, -1), (-2, 1), (1, -1), (1, 1), (-1, 1), (-1, -1)]
+WIDE_STEPS += [(0, -1), (0, 1), (-2, 0), (1, 0), (-1, 0)]
 
 
 def one_dimension():
@@ -226,6 +227,7 @@
     near,
     z_low,
     z_high,
+    x_face,
     slab_got,
     x_face_got,
     layer_got,
@@ -264,10 +266,10 @@
         (energy_forth_hbm, energy_forth),
         (energy_back_hbm, energy_back),
         (whole_forth_hbm, whole_forth),
-        (whole_back_hbm, whole_back),
         (widen_hbm, widen),
         (quad_weight_hbm, quad_weight),
         (whole_weight_hbm, whole_weight),
+        (whole_back_hbm, whole_back),
     ]
     loads = [
         pltpu.make_async_copy(source, target, in_sems.at[number])
@@ -285,7 +287,28 @@
 
     barrier = pltpu.get_barrier_semaphore()
     one_phase = n_dom * n_sub <= 64
-    if one_phase:
+    if one_phase and n_sub <= 4:
+        count = n_dom - 1
+        for dz in (-1, 1):
+            count = count + n_dom * inside(0, dz).astype(jnp.int32)
+        for dz in (0, -1, 1):
+
+            def greet(dz=dz):
+                @pl.loop(0 if dz else 1, n_dom, unroll=True)
+                def _(i):
+                    pl.semaphore_signal(
+                        barrier,
+                        inc=1,
+                        device_id=(lax.rem(dom + i, n_dom), sub + dz),
+                        device_id_type=MESH,
+                    )
+
+            if dz:
+                pl.when(inside(0, dz))(greet)
+            else:
+                greet()
+
+    elif one_phase:
         devices = n_dom * n_sub
         count = devices - 1
 
@@ -741,6 +764,18 @@
             for c in range(3)
         ]
 
+    def back_to_lattice(nodes):
+        for x in range(3):
+            for pair in range(8):
+                at = 16 * (x + 1) + 2 * pair
+                even = nodes[pl.ds(at, 3, stride=64), :]
+                odd = nodes[pl.ds(at + 1, 3, stride=64), :]
+                out_wide[8 * x : 8 * x + 3, 128 * pair : 128 * pair + 128] = even + turn(odd, 0, 64)
+        back = lax.dot_general(
+            split_three(out_wide[...]), pick[...], (((1,), (1,)), ((), ())), preferred_element_type=jnp.float32
+        )
+        return back[0:24] + back[24:48] + back[48:72]
+
     by_force, by_image = step * step * on_force, step * step * on_image
     jacobian = [
         [
@@ -770,26 +805,45 @@
             out = piece if out is None else out + piece
         return out + turn(out, 0, 64)
 
-    layer = lay([jnp.where(c_first, part[k], whole[k]) for k in comps], 0)
-    z_low[0:16] = lay([part[k][0:16] for k in comps], 0)
-    z_low[16:64] = layer[16:64]
-    z_low[64:80] = layer[0:16]
-    z_low[80:96] = lay([part[k][48:64] for k in comps], 0)
+    layer = [jnp.where(c_first, part[k], whole[k]) for k in comps]
+    right_half = jnp.logical_not(low_half)
+    r_here = r_of[:16]
+
+    def lay_group(fields, a):
+        out = None
+        half = low_half[:16] if a < 2 else right_half[:16]
+        for k in comps:
+            spot = 3 * (a % 2) + k
+            piece = jnp.where(
+                half & (r_here == spot), turn(fields[k], 0, 64 * (a // 2) + spot), 0.0
+            )
+            out = piece if out is None else out + piece
+        return out
+
+    groups = [lay_group([f[16 * a : 16 * a + 16] for f in layer], a) for a in range(4)]
+    upper_groups = groups[1] + groups[2] + groups[3]
+    face_part = lay_group([part[k][0:16] for k in comps], 0)
+    z_low[0] = turn(face_part + upper_groups, 0, 64)
+    z_low[1] = groups[0] + upper_groups
+    z_low[2] = lay([part[k][48:64] for k in comps], 0)
     z_high[...] = lay([ours[pl.ds(64 * k + 3, 16, stride=4), :] for k in comps], EZ - 1)
-
-    blocks = ours.reshape(3, 64, 128)
+    x_face[0, 0:16] = part[1][0:16] + turn(part[0][0:16], 0, 64)
+    x_face[0, 16:24] = part[2][8:16] + turn(part[2][0:8], 0, 64)
+    x_face[1, 0:16] = part[0][48:64] + turn(part[1][48:64], 0, 64)
+    x_face[1, 16:24] = part[2][48:56] + turn(part[2][56:64], 0, 64)
+
     routes = {
         (-1, 0): (near, slab_got),
-        (-2, 0): (blocks.at[:, pl.ds(0, 16)], x_face_got.at[0]),
-        (1, 0): (blocks.at[:, pl.ds(48, 16)], x_face_got.at[1]),
-        (0, -1): (z_low.at[pl.ds(16, 64)], layer_got.at[0]),
-        (-1, -1): (z_low.at[pl.ds(0, 64)], layer_got.at[1]),
-        (-2, -1): (z_low.at[pl.ds(0, 16)], edge_got.at[0]),
-        (1, -1): (z_low.at[pl.ds(80, 16)], edge_got.at[1]),
+        (-2, 0): (x_face.at[0], x_face_got.at[0]),
+        (1, 0): (x_face.at[1], x_face_got.at[1]),
+        (0, -1): (z_low.at[1], layer_got.at[0]),
+        (-1, -1): (z_low.at[0], layer_got.at[1]),
+        (-2, -1): (z_low.at[0], edge_got.at[0]),
+        (1, -1): (z_low.at[2], edge_got.at[1]),
         (0, 1): (z_high, floor_got.at[0]),
         (-1, 1): (z_high, floor_got.at[1]),
-        (-2, 1): (z_high, floor_got.at[2]),
-        (1, 1): (z_high, floor_got.at[3]),
+        (-2, 1): (z_high.at[pl.ds(0, 8)], floor_got.at[2, pl.ds(0, 8)]),
+        (1, 1): (z_high.at[pl.ds(8, 8)], floor_got.at[3, pl.ds(8, 8)]),
     }
     started = []
     for number, (dx, dz) in enumerate(WIDE_STEPS):
@@ -809,14 +863,15 @@
 
         started.append((wide_copy, (dx, dz)))
     exchange_wait(live_copies)
-    high_half = jnp.logical_not(low_half)
+    out_nodes[0:192, :] = new_velocity * owned
+    new_back = back_to_lattice(out_nodes)
     one_low, one_r = low_half[0:1], r_of[0:1]
     live_up = turn(live_got[0, 0:1, :], 0, 64)
     live_layer = live_got[1, 0:1, :] + turn(live_got[2, 0:1, :], 0, 64)
     live_wide = live_own[0:1, :] + live_up + jnp.where(one_r == EZ, turn(live_layer, 0, EZ), 0.0)
     wide_weight = whole_weight[...] * live_wide
     wide_wall = jnp.where(
-        jnp.logical_or(high_half, jnp.logical_or(a_of > 0, dom > 0))
+        jnp.logical_or(right_half, jnp.logical_or(a_of > 0, dom > 0))
         & jnp.logical_or(jnp.logical_or(c_of > 0, r_of > 0), sub > 0),
         1.0,
         0.0,
@@ -826,45 +881,53 @@
     exchange_wait(started)
     upper = slab_got[...]
     upper = jnp.concatenate([turn(upper, 0, 64), upper], axis=0)
-    layers = jnp.where(
-        low_half,
-        jnp.concatenate([layer_got[0, 48:64], layer_got[0, 0:48]], axis=0),
-        layer_got[1],
+    first_got, second_got = layer_got[0], layer_got[1]
+    mixed = (
+        jnp.where(low16, first_got, second_got),
+        jnp.where(low16, second_got, first_got),
     )
-    layers = layers + jnp.concatenate(
-        [
-            jnp.where(low16, edge_got[1], 0.0),
-            jnp.zeros((32, 128), jnp.float32),
-            jnp.where(low16, 0.0, edge_got[0]),
-        ],
-        axis=0,
-    )
+    right16 = right_half[:16]
+    edge_up = jnp.where(right16, edge_got[0], 0.0)
+    edge_down = jnp.where(low16, edge_got[1], 0.0)
     floor = jnp.where(low16, floor_got[0], floor_got[1])
-    floor = floor + jnp.where(jnp.logical_not(low16) & (row16 >= 12), turn(floor_got[2], 12, 0), 0.0)
+    floor = floor + jnp.where(right16 & (row16 >= 12), turn(floor_got[2], 12, 0), 0.0)
     floor = floor + jnp.where(low16 & (row16 < 4), turn(floor_got[3], 4, 0), 0.0)
+    face_low = [
+        x_face_got[1, 0:16],
+        turn(x_face_got[1, 0:16], 0, 64),
+        jnp.concatenate([x_face_got[1, 16:24], turn(x_face_got[1, 16:24], 0, 64)], axis=0),
+    ]
+    face_high = [
+        x_face_got[0, 0:16],
+        turn(x_face_got[0, 0:16], 0, 64),
+        jnp.concatenate([x_face_got[0, 16:24], turn(x_face_got[0, 16:24], 0, 64)], axis=0),
+    ]
     for k in comps:
         at = 64 * k
-        u = jnp.where(low_half, whole[k], upper[at : at + 64])
-        u = u + jnp.where(r_of == EZ, turn(layers, 0, EZ - k), 0.0)
-        wide_nodes[at : at + 64, :] = u
-        wide_nodes[at : at + 16, :] += x_face_got[1, k]
-        wide_nodes[at + 48 : at + 64, :] += turn(x_face_got[0, k], 0, 64)
+        rows = []
+        for a in range(4):
+            u = jnp.where(low16, whole[k][16 * a : 16 * a + 16], upper[at + 16 * a : at + 16 * a + 16])
+            spot = 3 * (a % 2) + k
+            piece = turn(mixed[a // 2], 0, EZ - spot - 64 * (a // 2))
+            if a == 0:
+                piece = piece + jnp.where(low16, turn(edge_down, 0, EZ - k), 0.0)
+                u = u + jnp.where(low16, face_low[k], 0.0)
+            if a == 3:
+                piece = piece + jnp.where(low16, 0.0, turn(edge_up, 0, EZ - k))
+                u = u + jnp.where(low16, 0.0, face_high[k])
+            rows.append(u + jnp.where(row16r == EZ, piece, 0.0))
+        wide_nodes[at : at + 64, :] = jnp.concatenate(rows, axis=0)
         below = pl.ds(at, 16, stride=4)
         above = pl.ds(at + 3, 16, stride=4)
         wide_nodes[below, :] += jnp.where(row16r == 0, turn(floor, 0, -k), 0.0)
-        wide_nodes[at + 48 : at + 64, :] += jnp.where(
-            low16, turn(wide_nodes[at : at + 16, :], 0, 64), 0.0
-        )
+        near_face = wide_nodes[at : at + 16, :]
+        far_face = wide_nodes[at + 48 : at + 64, :]
+        wide_nodes[at : at + 16, :] = near_face + jnp.where(low16, 0.0, turn(far_face, 0, 64))
+        wide_nodes[at + 48 : at + 64, :] = far_face + jnp.where(low16, turn(near_face, 0, 64), 0.0)
         tops = wide_nodes[above, :]
         bottoms = wide_nodes[below, :]
-        tops = tops + jnp.where(row16r == EZ - 1, turn(bottoms, 0, -1), 0.0)
-        wide_nodes[above, :] = tops
-        wide_nodes[below, :] = jnp.where(row16r == EZ, turn(tops, 0, 1), bottoms)
-        wide_nodes[at : at + 16, :] = jnp.where(
-            low16,
-            wide_nodes[at : at + 16, :],
-            turn(wide_nodes[at + 48 : at + 64, :], 0, 64),
-        )
+        wide_nodes[above, :] = tops + jnp.where(row16r == EZ - 1, turn(bottoms, 0, -1), 0.0)
+        wide_nodes[below, :] = bottoms + jnp.where(row16r == EZ, turn(tops, 0, 1), 0.0)
     relaxed = [wide_nodes[64 * k : 64 * k + 64, :] * wide_wall for k in comps]
     shaped = dot(whole_forth, jnp.concatenate(relaxed, axis=1))
     jacobian = [
@@ -887,24 +950,11 @@
     last = jnp.concatenate(last, axis=0)
     mesh_velocity = new_velocity - last / step
 
-    out_nodes[0:192, :] = new_velocity * owned
     out_nodes[192:384, :] = mesh_velocity * owned
+    mesh_back = back_to_lattice(out_nodes.at[pl.ds(192, 192)])
     for x in range(3):
-        for pair in range(8):
-            at = 16 * (x + 1) + 2 * pair
-            even = out_nodes[pl.ds(at, 6, stride=64), :]
-            odd = out_nodes[pl.ds(at + 1, 6, stride=64), :]
-            out_wide[8 * x : 8 * x + 6, 128 * pair : 128 * pair + 128] = even + turn(odd, 0, 64)
-    back = lax.dot_general(
-        split_three(out_wide[...]),
-        pick[...],
-        (((1,), (1,)), ((), ())),
-        preferred_element_type=jnp.float32,
-    )
-    back = back[0:24] + back[24:48] + back[48:72]
-    for x in range(3):
-        new_vel_out[:, plane * x : plane * (x + 1)] = back[8 * x : 8 * x + 3]
-        mesh_vel_out[:, plane * x : plane * (x + 1)] = back[8 * x + 3 : 8 * x + 6]
+        new_vel_out[:, plane * x : plane * (x + 1)] = new_back[8 * x : 8 * x + 3]
+        mesh_vel_out[:, plane * x : plane * (x + 1)] = mesh_back[8 * x : 8 * x + 3]
 
     for copy_of, size in late:
 
@@ -980,11 +1030,12 @@
             pltpu.SemaphoreType.DMA((6 + len(made_tables),)),
             pltpu.VMEM((192, 128), f32),
             pltpu.VMEM((96, 128), f32),
+            pltpu.VMEM((3, 16, 128), f32),
+            pltpu.VMEM((16, 128), f32),
+            pltpu.VMEM((2, 24, 128), f32),
             pltpu.VMEM((96, 128), f32),
-            pltpu.VMEM((16, 128), f32),
-            pltpu.VMEM((96, 128), f32),
-            pltpu.VMEM((2, 3, 16, 128), f32),
-            pltpu.VMEM((2, 64, 128), f32),
+            pltpu.VMEM((2, 24, 128), f32),
+            pltpu.VMEM((2, 16, 128), f32),
             pltpu.VMEM((2, 16, 128), f32),
             pltpu.VMEM((4, 16, 128), f32),
             pltpu.VMEM((192, 128), f32),

time: 33 us -> 31.5 us (0.955)
  Pallas kernels: 31.6 us -> 30 us
    pallas_call x1, Pallas kernels: 30.9 us -> 29.4 us  [body(): pl.pallas_call(functools.partial(kernel, n_dom, n_sub), out_shape=(pltpu....]
where the time goes in v3:
time: 31.5 us; the launch traced here: 31.3 us
  Pallas kernels  30 us (95%)
  between operations  1.29 us (4%)
    pallas_call x1, Pallas kernels, body(): pl.pallas_call(functools.partial(kernel, n_dom, n_sub), out_shape=(pltpu....  29.4 us
    pallas_call x1, Pallas kernels, body(): pl.pallas_call(hand_on, out_shape=[jax.ShapeDtypeStruct(m.shape, f32) for...  0.65 us

profile of v3, /device:TPU:0, one launch (start us, length us, event | category | flops | bytes accessed | tf_op | source)
XLA Modules:
  0.0 31.3 jit_solution(2383033262514659016)
XLA Ops:
  1.3 29.4 %shard_map.193 = (f32[3,1350]{1,0:T(4,128)S(1)}, f32[27,48]{1,0:T(8,128)S(1)}, f32[3,1350]{1,0:T(4,128)S(1)}) custom-call(f32[3,1350]{1,0:T(4,128)} %disp_in_hbm.1, f32[3,1350]{1,0:T(4,128)} %vel_in_hbm.1, f32[27,48]{1,0:T(8,128)} %energy_in_hbm.1, f32[48,125]{1,0:T(8,128)} %bitcast.4, s32[1,48]{1,0:T(1,128)} %bitcast.5, f32[1,1]{1,0:T(1,128)} %bitcast.3.step_in_hbm, ...), custom_call_target="tpu_custom_call" | custom-call | tf_op jit(solution)/shard_map/pallas_call | solution.py:989
  30.7 0.6 %shard_map.194 = (f32[3,1350]{1,0:T(4,128)}, f32[27,48]{1,0:T(8,128)}, f32[3,1350]{1,0:T(4,128)}) custom-call(f32[3,1350]{1,0:T(4,128)S(1)} %get-tuple-element.6.refs_0_, f32[27,48]{1,0:T(8,128)S(1)} %get-tuple-element.7.refs_1_, f32[3,1350]{1,0:T(4,128)S(1)} %get-tuple-element.8.refs_2_), custom_call_target="tpu_custom_call" | custom-call | tf_op jit(solution)/shard_map/pallas_call | solution.py:1057

commit v4 on v3

--- a/solution.py
+++ b/solution.py
@@ -20,7 +20,7 @@
 viscosity = 0.3
 mesh_step = 0.01
 MESH = pl.DeviceIdType.MESH
-STEPS = [(dx, dz) for dx in (-1, 0, 1) for dz in (-1, 0, 1) if (dx, dz) != (0, 0)]
+STEPS = [(-1, -1), (-1, 1), (1, -1), (1, 1), (0, -1), (0, 1), (-1, 0), (1, 0)]
 WIDE_STEPS = [(-2, -1), (-2, 1), (1, -1), (1, 1), (-1, 1), (-1, -1)]
 WIDE_STEPS += [(0, -1), (0, 1), (-2, 0), (1, 0), (-1, 0)]
 
@@ -275,9 +275,6 @@
         pltpu.make_async_copy(source, target, in_sems.at[number])
         for number, (source, target) in enumerate(held)
     ]
-    for load in loads:
-        load.start()
-
     x_first[...] = jnp.zeros_like(x_first)
     x_got[...] = jnp.zeros_like(x_got)
     z_got[...] = jnp.zeros_like(z_got)
@@ -346,6 +343,9 @@
             pl.semaphore_signal(
                 barrier, inc=1, device_id=(dom, lax.rem(sub + i, n_sub)), device_id_type=MESH
             )
+
+    for load in loads:
+        load.start()
 
     first[...] = jnp.zeros_like(first)
     density_pad[...] = jnp.zeros_like(density_pad)
@@ -688,51 +688,49 @@
 
     late = []
 
-    def all_sum(value, slots, size, place, target, sends, recvs, cover=None):
+    def all_sum(value, slots, targets, sends, recvs, cover=None):
         slots[0] = value
 
-        def copy_of(i):
+        def copy_of(source, target, device):
             return pltpu.make_async_remote_copy(
-                src_ref=slots.at[0],
-                dst_ref=slots.at[i],
-                send_sem=sends.at[i],
-                recv_sem=recvs.at[i],
-                device_id=target(lax.rem(place + i, size)),
+                src_ref=source,
+                dst_ref=target,
+                send_sem=sends.at[0],
+                recv_sem=recvs.at[0],
+                device_id=device,
                 device_id_type=MESH,
             )
 
-        @pl.loop(1, size, unroll=True)
-        def _(i):
-            copy_of(i).start()
+        for number, device in targets:
+            copy_of(slots.at[0], slots.at[number], device).start()
 
         out = cover() if cover else None
 
-        @pl.loop(1, size, unroll=True)
-        def _(i):
-            copy_of(i).wait_recv()
-
-        late.append((copy_of, size))
+        others = slots.at[pl.ds(1, len(targets))]
+        whole_sum = copy_of(others, others, targets[0][1])
+        whole_sum.wait_recv()
+        late.append(whole_sum)
         return jnp.sum(slots[...], axis=0), out
+
+    doms = [lax.rem(dom + i, n_dom) for i in range(n_dom)]
+    subs = [lax.rem(sub + i, n_sub) for i in range(n_sub)]
 
     def ahead():
         return [gradient(v) for v in (displacement + step * velocity, force, image)]
 
     if one_phase:
-        packed, slopes = all_sum(
-            packed,
-            sum_dom,
-            n_dom * n_sub,
-            dom * n_sub + sub,
-            lambda t: (t // n_sub, lax.rem(t, n_sub)),
-            dom_send,
-            dom_recv,
-            ahead,
-        )
+        targets = [
+            (j * n_dom + i, (doms[i], subs[j]))
+            for j in [*range(1, n_sub), 0]
+            for i in range(n_dom)
+            if i + j > 0
+        ]
+        packed, slopes = all_sum(packed, sum_dom, targets, dom_send, dom_recv, ahead)
     else:
-        packed, slopes = all_sum(
-            packed, sum_dom, n_dom, dom, lambda t: (t, sub), dom_send, dom_recv, ahead
-        )
-        packed, _ = all_sum(packed, sum_sub, n_sub, sub, lambda t: (dom, t), sub_send, sub_recv)
+        targets = [(i, (doms[i], sub)) for i in range(1, n_dom)]
+        packed, slopes = all_sum(packed, sum_dom, targets, dom_send, dom_recv, ahead)
+        targets = [(j, (dom, subs[j])) for j in range(1, n_sub)]
+        packed, _ = all_sum(packed, sum_sub, targets, sub_send, sub_recv)
     rr, rw, ww, wmw = (
         jnp.sum(jnp.where(lane1 == k, packed, 0.0), axis=1, keepdims=True) for k in range(4)
     )
@@ -877,6 +875,14 @@
         0.0,
     )
     low16, row16r = low_half[:16], r_of[:16]
+
+    for whole_sum in late:
+        whole_sum.wait_send()
+    for copy, (dx, dz) in waits + started:
+
+        @pl.when(inside(dx, dz))
+        def _():
+            copy.wait_send()
 
     exchange_wait(started)
     upper = slab_got[...]
@@ -955,18 +961,6 @@
     for x in range(3):
         new_vel_out[:, plane * x : plane * (x + 1)] = new_back[8 * x : 8 * x + 3]
         mesh_vel_out[:, plane * x : plane * (x + 1)] = mesh_back[8 * x : 8 * x + 3]
-
-    for copy_of, size in late:
-
-        @pl.loop(1, size, unroll=True)
-        def _(i, copy_of=copy_of):
-            copy_of(i).wait_send()
-
-    for copy, (dx, dz) in waits:
-
-        @pl.when(inside(dx, dz))
-        def _():
-            copy.wait_send()
 
 
 def hand_on(*refs):

time: 31.5 us -> 31 us (0.984)
  Pallas kernels: 30 us -> 29.6 us
    pallas_call x1, Pallas kernels: 29.4 us -> 28.9 us  [body(): pl.pallas_call(functools.partial(kernel, n_dom, n_sub), out_shape=(pltpu....]
where the time goes in v4:
time: 31 us; the launch traced here: 30.9 us
  Pallas kernels  29.6 us (95%)
  between operations  1.29 us (4%)
    pallas_call x1, Pallas kernels, body(): pl.pallas_call(functools.partial(kernel, n_dom, n_sub), out_shape=(pltpu....  28.9 us
    pallas_call x1, Pallas kernels, body(): pl.pallas_call(hand_on, out_shape=[jax.ShapeDtypeStruct(m.shape, f32) for...  0.65 us

profile of v4, /device:TPU:0, one launch (start us, length us, event | category | flops | bytes accessed | tf_op | source)
XLA Modules:
  0.0 30.9 jit_solution(7146294252912930537)
XLA Ops:
  1.3 28.9 %shard_map.193 = (f32[3,1350]{1,0:T(4,128)S(1)}, f32[27,48]{1,0:T(8,128)S(1)}, f32[3,1350]{1,0:T(4,128)S(1)}) custom-call(f32[3,1350]{1,0:T(4,128)} %disp_in_hbm.1, f32[3,1350]{1,0:T(4,128)} %vel_in_hbm.1, f32[27,48]{1,0:T(8,128)} %energy_in_hbm.1, f32[48,125]{1,0:T(8,128)} %bitcast.4, s32[1,48]{1,0:T(1,128)} %bitcast.5, f32[1,1]{1,0:T(1,128)} %bitcast.3.step_in_hbm, ...), custom_call_target="tpu_custom_call" | custom-call | tf_op jit(solution)/shard_map/pallas_call | solution.py:983
  30.2 0.6 %shard_map.194 = (f32[3,1350]{1,0:T(4,128)}, f32[27,48]{1,0:T(8,128)}, f32[3,1350]{1,0:T(4,128)}) custom-call(f32[3,1350]{1,0:T(4,128)S(1)} %get-tuple-element.6.refs_0_, f32[27,48]{1,0:T(8,128)S(1)} %get-tuple-element.7.refs_1_, f32[3,1350]{1,0:T(4,128)S(1)} %get-tuple-element.8.refs_2_), custom_call_target="tpu_custom_call" | custom-call | tf_op jit(solution)/shard_map/pallas_call | solution.py:1051

commit v5 on v4

--- a/solution.py
+++ b/solution.py
@@ -80,7 +80,8 @@
     ]
     grad = np.concatenate([halves(t, 64) for t in triples], axis=0)
     whole = [np.concatenate([t, np.repeat(t[-1:], 3, axis=0)], axis=0) for t in triples]
-    basis = halves(outer_triple(values, values, values), 64)
+    basis = outer_triple(values, values, values)
+    basis = np.concatenate([basis, np.repeat(basis[-1:], 3, axis=0)], axis=0)
     energy = halves(outer_triple(bernstein, bernstein, bernstein), 32)
     weight = np.einsum("i,j,k->ijk", weights, weights, weights).reshape(125)
     weight = np.pad(weight, (0, 3))
@@ -472,8 +473,6 @@
         waits.extend(started)
 
     def exchange_add(rnd, source, target, fields, x_from, ups, downs):
-        if target is not source:
-            target[...] = source[...]
         top = lax.broadcasted_iota(jnp.int32, (8, 128), 0) < 4
         for came, side, place in ((ups, 0, 0), (downs, 1, 3)):
             if not came:
@@ -534,7 +533,7 @@
     mass_density = by_point[0:64] + turn(by_point[64:128], 0, 64)
     weight = quad_weight[...]
     live_weight = weight * live
-    mass_weight = live_weight * mass_density
+    mass_weight = whole_weight[...] * (live_own[0:1, :] * by_point)
     at_points = dot(energy_forth, jnp.concatenate([by_lane, turn(by_lane, 0, 64)], axis=0))
 
     def paired(v):
@@ -580,7 +579,7 @@
         return v
 
     def interpolate(v):
-        return dot(basis_forth, paired(v))
+        return dot(basis_forth, jnp.concatenate([v[0:64], v[64:128], v[128:192]], axis=1))
 
     def volume_of(jacobian, cofactor):
         return (
@@ -592,6 +591,7 @@
     def begin(rnd, v, ups=True, downs=True):
         source = local.at[rnd - 1]
         source[...] = v
+        state[...] = v
         return exchange_start(rnd, source, 3, lambda slot: x_got.at[rnd - 1, slot], ups, downs)
 
     def finish(rnd, started, ups=True, downs=True):
@@ -602,8 +602,8 @@
         )
         return state[...] * off_wall
 
+    out_nodes[...] = first[0:384, :]
     exchange_wait(started)
-    out_nodes[...] = first[0:384, :]
     exchange_add(0, out_nodes, out_nodes, 6, lambda slot: x_first, True, False)
     displacement = out_nodes[0:192, :]
     velocity = out_nodes[192:384, :]
@@ -662,7 +662,10 @@
     wide_mass = jnp.concatenate([mass_weight] * 3, axis=1)
     values = interpolate(force)
     weighted = wide_mass * values
-    image = share(jnp.concatenate(folded(dot(basis_back, weighted)), axis=0))
+    product = dot(basis_back, weighted)
+    image = share(
+        jnp.concatenate([product[:, 128 * k : 128 * k + 128] for k in range(3)], axis=0)
+    )
     started = begin(2, image)
 
     def total(x):

time: 31 us -> 30.8 us (level)
  no operation moved by 1% of the time
where the time goes in v5:
time: 30.8 us; the launch traced here: 30.6 us
  Pallas kernels  29.3 us (95%)
  between operations  1.29 us (4%)
    pallas_call x1, Pallas kernels, body(): pl.pallas_call(functools.partial(kernel, n_dom, n_sub), out_shape=(pltpu....  28.7 us
    pallas_call x1, Pallas kernels, body(): pl.pallas_call(hand_on, out_shape=[jax.ShapeDtypeStruct(m.shape, f32) for...  0.65 us

profile of v5, /device:TPU:0, one launch (start us, length us, event | category | flops | bytes accessed | tf_op | source)
XLA Modules:
  0.0 30.6 jit_solution(4749421656469552428)
XLA Ops:
  1.3 28.7 %shard_map.193 = (f32[3,1350]{1,0:T(4,128)S(1)}, f32[27,48]{1,0:T(8,128)S(1)}, f32[3,1350]{1,0:T(4,128)S(1)}) custom-call(f32[3,1350]{1,0:T(4,128)} %disp_in_hbm.1, f32[3,1350]{1,0:T(4,128)} %vel_in_hbm.1, f32[27,48]{1,0:T(8,128)} %energy_in_hbm.1, f32[48,125]{1,0:T(8,128)} %bitcast.4, s32[1,48]{1,0:T(1,128)} %bitcast.5, f32[1,1]{1,0:T(1,128)} %bitcast.3.step_in_hbm, ...), custom_call_target="tpu_custom_call" | custom-call | tf_op jit(solution)/shard_map/pallas_call | solution.py:986
  30.0 0.6 %shard_map.194 = (f32[3,1350]{1,0:T(4,128)}, f32[27,48]{1,0:T(8,128)}, f32[3,1350]{1,0:T(4,128)}) custom-call(f32[3,1350]{1,0:T(4,128)S(1)} %get-tuple-element.6.refs_0_, f32[27,48]{1,0:T(8,128)S(1)} %get-tuple-element.7.refs_1_, f32[3,1350]{1,0:T(4,128)S(1)} %get-tuple-element.8.refs_2_), custom_call_target="tpu_custom_call" | custom-call | tf_op jit(solution)/shard_map/pallas_call | solution.py:1054

commit v6 on v5

--- a/solution.py
+++ b/solution.py
@@ -361,8 +361,6 @@
     low_half = lane < HALF
     valid = low_half & (r_of < EZ)
     triple = lambda x: jnp.concatenate([x, x, x], axis=0)
-    y_up = triple((b_of == 3) & (q_of < EY - 1) & valid)
-    y_down = triple((b_of == 0) & (q_of > 0) & valid)
     z_up = triple((c_of == 3) & (r_of < EZ - 1) & valid)
     z_down = triple((c_of == 0) & (r_of > 0) & valid)
     off_wall = jnp.where(
@@ -574,7 +572,17 @@
 
     def share(v):
         v = v * jnp.where(triple(valid), 1.0, 0.0)
-        v = v + jnp.where(y_up, turn(v, 12, -ROW), 0.0) + jnp.where(y_down, turn(v, -12, ROW), 0.0)
+        first_rows = row[:8] < 4
+        here = valid[:8]
+        up = jnp.logical_not(first_rows) & (q_of[:8] < EY - 1) & here
+        down = first_rows & (q_of[:8] > 0) & here
+        rows = []
+        for at in range(0, 192, 16):
+            near_rows, far_rows = v[at : at + 8], v[at + 8 : at + 16]
+            swapped = turn(jnp.where(first_rows, near_rows, far_rows), 4, 0)
+            rows.append(near_rows + jnp.where(down, turn(swapped, 0, ROW), 0.0))
+            rows.append(far_rows + jnp.where(up, turn(swapped, 0, -ROW), 0.0))
+        v = jnp.concatenate(rows, axis=0)
         v = v + jnp.where(z_up, turn(v, 3, -1), 0.0) + jnp.where(z_down, turn(v, -3, 1), 0.0)
         return v
 

time: 30.8 us -> 30.8 us (level)
  no operation moved by 1% of the time
where the time goes in v6:
time: 30.8 us; the launch traced here: 30.6 us
  Pallas kernels  29.4 us (95%)
  between operations  1.29 us (4%)
    pallas_call x1, Pallas kernels, body(): pl.pallas_call(functools.partial(kernel, n_dom, n_sub), out_shape=(pltpu....  28.7 us
    pallas_call x1, Pallas kernels, body(): pl.pallas_call(hand_on, out_shape=[jax.ShapeDtypeStruct(m.shape, f32) for...  0.65 us

profile of v6, /device:TPU:0, one launch (start us, length us, event | category | flops | bytes accessed | tf_op | source)
XLA Modules:
  0.0 30.6 jit_solution(12154384782072631341)
XLA Ops:
  1.3 28.7 %shard_map.193 = (f32[3,1350]{1,0:T(4,128)S(1)}, f32[27,48]{1,0:T(8,128)S(1)}, f32[3,1350]{1,0:T(4,128)S(1)}) custom-call(f32[3,1350]{1,0:T(4,128)} %disp_in_hbm.1, f32[3,1350]{1,0:T(4,128)} %vel_in_hbm.1, f32[27,48]{1,0:T(8,128)} %energy_in_hbm.1, f32[48,125]{1,0:T(8,128)} %bitcast.4, s32[1,48]{1,0:T(1,128)} %bitcast.5, f32[1,1]{1,0:T(1,128)} %bitcast.3.step_in_hbm, ...), custom_call_target="tpu_custom_call" | custom-call | tf_op jit(solution)/shard_map/pallas_call | solution.py:994
  30.0 0.6 %shard_map.194 = (f32[3,1350]{1,0:T(4,128)}, f32[27,48]{1,0:T(8,128)}, f32[3,1350]{1,0:T(4,128)}) custom-call(f32[3,1350]{1,0:T(4,128)S(1)} %get-tuple-element.6.refs_0_, f32[27,48]{1,0:T(8,128)S(1)} %get-tuple-element.7.refs_1_, f32[3,1350]{1,0:T(4,128)S(1)} %get-tuple-element.8.refs_2_), custom_call_target="tpu_custom_call" | custom-call | tf_op jit(solution)/shard_map/pallas_call | solution.py:1062
